TPU v7x, 256 devices: a whole 4x4x8 slice. The times are simulated.
256 devices in a mesh: cp: 64 (over y, z, core), fs: 4 (over x).
Axes of the slice: x: 4, y: 4, z: 8, core: 2. Of those that a mesh axis runs over, the one named last changes fastest.
Arguments:
- embeds: bfloat16 [4, 16384, 4096], P('fs', 'cp'), may hold values from -16 to 16
- queries: bfloat16 [4, 16384, 2048], P('fs', 'cp'), may hold values from -12 to 12
- key_heads: bfloat16 [4, 16384, 512], P('fs', 'cp'), may hold values from -4 to 4
- cotangent: bfloat16 [4, 16384, 2048], P('fs', 'cp'), may hold values from -6 to 6
- doc_start: int32 [4, 16384], P('fs', 'cp'), may hold values from 0 to 16383, as said below
- need_ids: int32 [4, 64, 5], P('fs', 'cp'), may hold values from -1 to 63, as said below
- y_weight: bfloat16 [4096, 512], P(('cp', 'fs')), may hold values from -0.09375 to 0.09375
- z_weight: float32 [4096, 512], P(('cp', 'fs')), may hold values from -0.09375 to 0.09375
- x_weight: float32 [4096, 512], P(('cp', 'fs')), may hold values from -0.09375 to 0.09375
- second_moment: float32 [4096, 512], P(('cp', 'fs')), may hold values from 1e-05 to 0.001
Outputs:
- z_next: float32 [4096, 512], P(('cp', 'fs'))
- x_next: float32 [4096, 512], P(('cp', 'fs'))
- moment_next: float32 [4096, 512], P(('cp', 'fs'))
- y_next: bfloat16 [4096, 512], P(('cp', 'fs'))
Inputs may be any that keep to these rules, and one draw needn't show every extreme that they name: `doc_start`: documents are contiguous and hold at most 1024 tokens, so a query block needs key-value blocks at most 4 blocks back; in every sequence some query block needs the block exactly 4 back. need_ids[f, b, j] is b - j when some query of block b is allowed a key of block b - j, else -1; need_ids[f, b, 0] is always b.
All inputs are finite; a program needn't handle non-finite values.
Results may differ from a plain program's by a relative error of at most 0.0027.
The roundings to bfloat16 on the way count: a program that leaves them out, or rounds other values in their place, can miss the bound.
Values may be sent and summed in bfloat16 or wider, within the bound.
A program may use at most 128 MiB of HBM per device.

v0:
```python
import math

import jax
import jax.numpy as jnp
from jax import lax
from jax.sharding import Mesh
from jax.sharding import PartitionSpec as P

HEAD = 128
KV_HEADS = 4
WIN = 4
GROUP = 4
CP = ("cp_0", "cp_1", "cp_2")
CP_FS = ("cp_0", "cp_1", "cp_2", "fs")


NORM_EPS = 0.01
MOMENT_DECAY = 0.95
LEARN_RATE = 0.005
WEIGHT_DECAY = 0.1
ADAM_EPS = 1e-08
AVERAGE_MIX = 0.25
INTERP_BETA = 0.9


def joined_along(parts, dim):
    parts = jnp.moveaxis(parts, 0, dim)
    shape = parts.shape
    return parts.reshape(*shape[:dim], shape[dim] * shape[dim + 1], *shape[dim + 2 :])


def gather_in_order(shard, axes, sequence):
    parts = shard
    for k in sequence:
        parts = lax.all_gather(parts, axes[k])
    done = sequence[::-1]
    back = [done.index(k) for k in range(len(axes))]
    parts = parts.transpose(*back, *range(len(axes), parts.ndim))
    return parts.reshape(-1, *shard.shape)


def whole_of(shard, axes, sequence, dim):
    return joined_along(gather_in_order(shard, axes, sequence), dim)


def from_behind(block, axis, distance):
    devices = range(lax.axis_size(axis))
    route = [(i - distance, i) for i in devices if i - distance in devices]
    return lax.ppermute(block, axis, route)


def as_sent(shard):

    def short(part):
        return part.astype(jnp.bfloat16) if part.dtype == jnp.float32 else part

    return jax.tree.map(short, shard)


def from_everyone(shard, axis):
    count = lax.axis_size(axis)
    return lax.all_to_all(
        jnp.broadcast_to(shard[None], (count, *shard.shape)), axis, 0, 0, tiled=True
    )


def gather_directly(shard, axis, dim):
    parts = from_everyone(shard, axis)
    return joined_along(parts, dim)


def cut_along(shard, dim, count):
    before, after = (shard.shape[:dim], shard.shape[dim + 1 :])
    return jnp.moveaxis(shard.reshape(*before, count, -1, *after), dim, 0)


def sum_at_owner(shard, axis, dim):
    parts = cut_along(shard, dim, lax.axis_size(axis))
    arrived = lax.all_to_all(parts, axis, split_axis=0, concat_axis=0, tiled=True)
    return arrived.sum(axis=0)


def visible(doc_rows, need_row, block_id, tok_rows):
    span_rows = (WIN + 1) * tok_rows
    query_pos = block_id * tok_rows + jnp.arange(tok_rows, dtype=jnp.int32)
    key_pos = (block_id - WIN) * tok_rows + jnp.arange(span_rows, dtype=jnp.int32)
    key_block = block_id - WIN + jnp.arange(span_rows, dtype=jnp.int32) // tok_rows
    listed = jnp.any(need_row[None, :] == key_block[:, None], axis=1)
    return (
        (key_pos[None, :] >= doc_rows[:, None])
        & (key_pos[None, :] <= query_pos[:, None])
        & listed[None, :]
    )


def block_attention(query_rows, key_window, value_window, allowed):
    tok_rows = query_rows.shape[0]
    scaling = 1.0 / math.sqrt(HEAD)
    query_split = query_rows.reshape(tok_rows, KV_HEADS, GROUP, HEAD)
    prob_list = []
    out_list = []
    for kv_head in range(KV_HEADS):
        key_part = key_window[:, kv_head * HEAD : (kv_head + 1) * HEAD]
        value_part = value_window[:, kv_head * HEAD : (kv_head + 1) * HEAD]
        scores = (
            jnp.einsum(
                "tgh,sh->gts", query_split[:, kv_head], key_part, preferred_element_type=jnp.float32
            )
            * scaling
        )
        scores = jnp.where(allowed[None], scores, -jnp.inf)
        largest = jnp.max(scores, axis=-1, keepdims=True)
        weights = jnp.exp(scores - largest)
        probs_low = (weights / jnp.sum(weights, axis=-1, keepdims=True)).astype(jnp.bfloat16)
        prob_list.append(probs_low)
        out_list.append(
            jnp.einsum("gts,sh->tgh", probs_low, value_part, preferred_element_type=jnp.float32)
        )
    attended = jnp.stack(out_list, axis=1).reshape(tok_rows, KV_HEADS * GROUP * HEAD)
    return (prob_list, attended)


def norm_backward(attended, cot_rows, token_total):
    square_mean = jnp.mean(attended * attended, axis=-1, keepdims=True) + NORM_EPS
    root_scale = jnp.sqrt(square_mean)
    normed = attended / root_scale
    upstream = cot_rows.astype(jnp.float32) / token_total
    inner = jnp.mean(upstream * normed, axis=-1, keepdims=True)
    return ((upstream - normed * inner) / root_scale).astype(jnp.bfloat16)


def window_grads(prob_list, out_grad):
    tok_rows = out_grad.shape[0]
    grad_split = out_grad.reshape(tok_rows, KV_HEADS, GROUP, HEAD)
    head_parts = []
    for kv_head in range(KV_HEADS):
        head_parts.append(
            jnp.einsum(
                "gts,tgh->sh",
                prob_list[kv_head],
                grad_split[:, kv_head],
                preferred_element_type=jnp.float32,
            )
        )
    return jnp.concatenate(head_parts, axis=1)


def on_device(
    embeds,
    queries,
    key_heads,
    cotangent,
    doc_start,
    need_ids,
    y_weight,
    z_weight,
    x_weight,
    second_moment,
):
    tokens_here = embeds[0]
    tok_rows = tokens_here.shape[0]
    kv_width = key_heads.shape[2]
    block_id = lax.axis_index(CP)
    token_total = tok_rows * lax.axis_size(CP) * lax.axis_size("fs")
    columns = tokens_here
    values = jnp.dot(
        columns, whole_of(y_weight, CP_FS, (0, 1, 3, 2), 0), preferred_element_type=jnp.float32
    ).astype(jnp.bfloat16)
    paired = jnp.concatenate([key_heads[0], values], axis=1)
    stacked = paired[None]
    filled = 1
    while filled < WIN + 1:
        amount = min(filled, WIN + 1 - filled)
        arrived = from_behind(stacked[:amount], CP, filled)
        stacked = jnp.concatenate([stacked, arrived], axis=0)
        filled = filled + amount
    window = stacked[::-1].reshape((WIN + 1) * tok_rows, 2 * kv_width)
    allowed = visible(doc_start[0], need_ids[0, 0], block_id, tok_rows)
    prob_list, attended = block_attention(
        queries[0], window[:, :kv_width], window[:, kv_width:], allowed
    )
    out_grad = norm_backward(attended, cotangent[0], token_total)
    shares = window_grads(prob_list, out_grad).reshape(WIN + 1, tok_rows, kv_width)[::-1]
    slots = [shares[remain] for remain in range(WIN + 1)]
    distance = 1
    while distance <= WIN:
        moving = [
            remain for remain in range(WIN + 1) if remain & distance and slots[remain] is not None
        ]
        arrived = from_behind(
            as_sent(jnp.stack([slots[remain] for remain in moving])), CP, -distance
        )
        for position, remain in enumerate(moving):
            slots[remain - distance] = slots[remain - distance] + arrived[position]
            slots[remain] = None
        distance = distance * 2
    grad_total = slots[0]
    value_grad = grad_total.astype(jnp.bfloat16)
    own_rows = y_weight.shape[0]
    fs_count = lax.axis_size("fs")
    cp_count = lax.axis_size(CP)
    split_cols = tokens_here.reshape(tok_rows, cp_count, fs_count * own_rows)
    exchanged = lax.all_to_all(split_cols, "fs", split_axis=2, concat_axis=0, tiled=True)
    group_cols = exchanged.reshape(fs_count * tok_rows, cp_count * own_rows)
    group_grads = gather_directly(value_grad, "fs", 0)
    columns = group_cols
    gradient = sum_at_owner(
        lax.dot_general(
            columns, group_grads, (((0,), (0,)), ((), ())), preferred_element_type=jnp.float32
        ),
        CP,
        0,
    )
    moment_next = MOMENT_DECAY * second_moment + (1.0 - MOMENT_DECAY) * gradient * gradient
    z_next = z_weight - LEARN_RATE * (
        gradient / (jnp.sqrt(moment_next) + ADAM_EPS) + WEIGHT_DECAY * y_weight.astype(jnp.float32)
    )
    x_next = (1.0 - AVERAGE_MIX) * x_weight + AVERAGE_MIX * z_next
    y_next = ((1.0 - INTERP_BETA) * z_next + INTERP_BETA * x_next).astype(jnp.bfloat16)
    return (z_next, x_next, moment_next, y_next)


def solution(mesh):
    finer = Mesh(mesh.devices.reshape(4, 8, 2, mesh.shape["fs"]), ("cp_0", "cp_1", "cp_2", "fs"))
    return jax.shard_map(
        on_device,
        mesh=finer,
        in_specs=(
            P("fs", CP, None),
            P("fs", CP, None),
            P("fs", CP, None),
            P("fs", CP, None),
            P("fs", CP),
            P("fs", CP, None),
            P(CP_FS, None),
            P(CP_FS, None),
            P(CP_FS, None),
            P(CP_FS, None),
        ),
        out_specs=(P(CP_FS, None), P(CP_FS, None), P(CP_FS, None), P(CP_FS, None)),
        check_vma=False,
    )
```

profile of v0, /device:TPU:1, one launch (start us, length us, event | category | flops | bytes accessed | tf_op | source)
XLA Modules:
  0.0 351.6 jit_solution(8123608670017165805)
XLA Ops:
  7.2 10.6 %all-gather = bf16[64,512]{1,0:T(8,128)(2,1)S(1)} all-gather(bf16[16,512]{1,0:T(8,128)(2,1)} %param.16), channel_id=2, replica_groups=mesh['cp_0'=4,'cp_1'=8,'cp_2'=2,'fs'=4] {'cp_0'}, dimensions={0}, use_global_device_ids=true | all-gather | bytes 81920 | tf_op jit(solution)/shard_map/all_gather | solution.py:35
  17.8 24.8 %all-gather.1 = bf16[32,16,512]{2,1,0:T(8,128)(2,1)} all-gather(bf16[4,16,512]{2,1,0:T(8,128)(2,1)S(1)} %bitcast.250), channel_id=3, replica_groups=mesh['cp_0'=4,'cp_1'=8,'cp_2'=2,'fs'=4] {'cp_1'}, dimensions={0}, use_global_device_ids=true | all-gather | bytes 589824 | tf_op jit(solution)/shard_map/all_gather | solution.py:35
  42.7 40.8 %all-gather.7.cloned.1.call-done = bf16[32,4,16,512]{3,2,1,0:T(8,128)(2,1)} async-done(((bf16[8,4,16,512]{3,2,1,0:T(8,128)(2,1)}), bf16[32,4,16,512]{3,2,1,0:T(8,128)(2,1)}) %all-gather.7.cloned.1.call-update) | async-done | bytes 2097168 | tf_op jit(solution)/shard_map/all_gather | solution.py:35
  83.5 21.7 %all-gather.9.cloned.1.call-done = bf16[8,8,4,16,512]{4,3,2,1,0:T(8,128)(2,1)} async-done(((bf16[4,8,4,16,512]{4,3,2,1,0:T(8,128)(2,1)}), bf16[8,8,4,16,512]{4,3,2,1,0:T(8,128)(2,1)}) %all-gather.9.cloned.1.call-update) | async-done | bytes 4194320 | tf_op jit(solution)/shard_map/all_gather | solution.py:35
  105.3 2.7 copy.102
  109.3 3.0 collective-permute-start
  112.3 3.3 copy.123
  115.6 2.5 copy.124
  118.1 4.4 %all-to-all-start.1 = ((bf16[256,64,64]{0,1,2:T(8,128)(2,1)}), bf16[256,64,64]{0,1,2:T(8,128)(2,1)}, u32[]{:S(2)}, u32[]{:S(2)}) async-start(bf16[256,64,64]{0,1,2:T(8,128)(2,1)} %copy.124), calls=%async_computation.1 | async-start | bytes 4194304 | tf_op jit(solution)/shard_map/all_to_all | solution.py:203
  123.6 4.2 %collective-permute-start.1 = (bf16[2,256,1024]{2,1,0:T(8,128)(2,1)}, bf16[2,256,1024]{2,1,0:T(8,128)(2,1)}, u32[]{:S(2)}, u32[]{:S(2)}) collective-permute-start(bf16[2,256,1024]{2,1,0:T(8,128)(2,1)} %pad_maximum_fusion.3), channel_id=1, source_target_pairs={{0,8},{4,12},{8,16},{12,20},{16,24},{20,28},{24,32},{28,36},{32,40... | collective-permute-start | bytes 3145736 | tf_op jit(solution)/shard_map/ppermute | solution.py:49
  128.0 2.3 copy.103
  130.3 1.9 copy.105
  132.3 4.4 %collective-permute-start.2 = (bf16[1,256,1024]{2,1,0:T(8,128)(2,1)S(1)}, bf16[1,256,1024]{2,1,0:T(8,128)(2,1)S(1)}, u32[]{:S(2)}, u32[]{:S(2)}) collective-permute-start(bf16[1,256,1024]{2,1,0:T(8,128)(2,1)S(1)} %maximum_bitcast_fusion), channel_id=1, source_target_pairs={{0,16},{4,20},{8,24},{12,28},{16,32},{20,36},{24,40},{28,44},{32,4... | collective-permute-start | bytes 1572872 | tf_op jit(solution)/shard_map/ppermute | solution.py:49
  137.8 24.5 %collective-permute-done.2 = bf16[1,256,1024]{2,1,0:T(8,128)(2,1)S(1)} collective-permute-done((bf16[1,256,1024]{2,1,0:T(8,128)(2,1)S(1)}, bf16[1,256,1024]{2,1,0:T(8,128)(2,1)S(1)}, u32[]{:S(2)}, u32[]{:S(2)}) %collective-permute-start.2) | collective-permute-done | bytes 524320 | tf_op jit(solution)/shard_map/ppermute | solution.py:49
  164.0 1.8 rev.4
  165.7 5.2 %exponential_reduce_fusion.3 = (f32[4,256]{1,0:T(4,128)S(1)}, f32[4,256,1280]{1,2,0:T(8,128)}) fusion(pred[256,1280]{0,1:T(8,128)(4,1)S(1)} %and_and_fusion, bf16[1280,1024]{1,0:T(8,128)(2,1)} %bitcast.229, bf16[256,4,4,128]{0,3,2,1:T(8,128)(2,1)} %bitcast.245), kind=kOutput, calls=%fused_computation.19 | convolution fusion | flops 340788480 | bytes 6164480 | tf_op jit(solution)/shard_map/sub | solution.py:113
  170.9 5.1 %exponential_reduce_fusion.2 = (f32[4,256]{1,0:T(4,128)S(1)}, f32[4,256,1280]{1,2,0:T(8,128)}) fusion(pred[256,1280]{0,1:T(8,128)(4,1)S(1)} %and_and_fusion, bf16[1280,1024]{1,0:T(8,128)(2,1)} %bitcast.230, bf16[256,4,4,128]{0,3,2,1:T(8,128)(2,1)S(1)} %bitcast.246), kind=kOutput, calls=%fused_computation.18 | convolution fusion | flops 340788480 | bytes 6164480 | tf_op jit(solution)/shard_map/sub | solution.py:113
  176.1 5.1 %exponential_reduce_fusion.1 = (f32[4,256]{1,0:T(4,128)S(1)}, f32[4,256,1280]{1,2,0:T(8,128)}) fusion(pred[256,1280]{0,1:T(8,128)(4,1)S(1)} %and_and_fusion, bf16[1280,1024]{1,0:T(8,128)(2,1)} %bitcast.231, bf16[256,4,4,128]{0,3,2,1:T(8,128)(2,1)S(1)} %bitcast.247), kind=kOutput, calls=%fused_computation.17 | convolution fusion | flops 340788480 | bytes 6164480 | tf_op jit(solution)/shard_map/sub | solution.py:113
  181.2 5.1 %exponential_reduce_fusion = (f32[4,256]{1,0:T(4,128)S(1)}, f32[4,256,1280]{1,2,0:T(8,128)}) fusion(pred[256,1280]{0,1:T(8,128)(4,1)S(1)} %and_and_fusion, bf16[1280,1024]{1,0:T(8,128)(2,1)} %bitcast.232, bf16[256,4,4,128]{0,3,2,1:T(8,128)(2,1)S(1)} %bitcast.248), kind=kOutput, calls=%fused_computation.16 | convolution fusion | flops 340788480 | bytes 6164480 | tf_op jit(solution)/shard_map/sub | solution.py:113
  186.3 4.0 %divide_convert_fusion.3 = bf16[4,256,1280]{1,2,0:T(8,128)(2,1)S(1)} fusion(f32[4,256,1280]{1,2,0:T(8,128)} %get-tuple-element.20, f32[4,256]{1,0:T(4,128)S(1)} %get-tuple-element.19), kind=kLoop, calls=%fused_computation.15 | loop fusion | flops 2621440 | bytes 7868416 | tf_op jit(solution)/shard_map/convert_element_type | solution.py:114
  190.8 4.0 %divide_convert_fusion.2 = bf16[4,256,1280]{1,2,0:T(8,128)(2,1)S(1)} fusion(f32[4,256,1280]{1,2,0:T(8,128)} %get-tuple-element.18, f32[4,256]{1,0:T(4,128)S(1)} %get-tuple-element.17), kind=kLoop, calls=%fused_computation.14 | loop fusion | flops 2621440 | bytes 7868416 | tf_op jit(solution)/shard_map/convert_element_type | solution.py:114
  203.2 2.9 copy.117
  206.1 2.5 fusion.8
  216.8 1.9 collective-permute-start.3
  220.2 16.3 %collective-permute-done.3 = bf16[2,256,512]{1,2,0:T(8,128)(2,1)S(1)} collective-permute-done((bf16[2,256,512]{1,2,0:T(8,128)(2,1)S(1)}, bf16[2,256,512]{1,2,0:T(8,128)(2,1)S(1)}, u32[]{:S(2)}, u32[]{:S(2)}) %collective-permute-start.3) | collective-permute-done | bytes 524320 | tf_op jit(solution)/shard_map/ppermute | solution.py:49
  237.9 10.1 %collective-permute-done.4 = bf16[1,256,512]{1,2,0:T(8,128)(2,1)S(1)} collective-permute-done((bf16[1,256,512]{1,2,0:T(8,128)(2,1)S(1)}, bf16[1,256,512]{1,2,0:T(8,128)(2,1)S(1)}, u32[]{:S(2)}, u32[]{:S(2)}) %collective-permute-start.4) | collective-permute-done | bytes 262176 | tf_op jit(solution)/shard_map/ppermute | solution.py:49
  249.4 4.7 %all-to-all-start = ((bf16[4,256,512]{2,1,0:T(8,128)(2,1)}), bf16[4,256,512]{2,1,0:T(8,128)(2,1)S(1)}, u32[]{:S(2)}, u32[]{:S(2)}) async-start(bf16[4,256,512]{2,1,0:T(8,128)(2,1)} %broadcast_in_dim.58), calls=%async_computation | async-start | bytes 2097152 | tf_op jit(solution)/shard_map/all_to_all | solution.py:62
  254.1 3.2 copy.126
  257.8 11.6 %all-to-all-done = bf16[4,256,512]{2,1,0:T(8,128)(2,1)S(1)} async-done(((bf16[4,256,512]{2,1,0:T(8,128)(2,1)}), bf16[4,256,512]{2,1,0:T(8,128)(2,1)S(1)}, u32[]{:S(2)}, u32[]{:S(2)}) %all-to-all-start) | async-done | bytes 1048608 | tf_op jit(solution)/shard_map/all_to_all | solution.py:62
  269.4 2.6 convolution_bitcast_fusion.4
  272.1 2.9 copy.127
  275.0 68.9 %all_to_all.25 = f32[64,16,512]{2,1,0:T(8,128)S(1)} all-to-all(f32[64,16,512]{2,1,0:T(8,128)} %bitcast.227), channel_id=1, replica_groups=mesh['cp_0'=4,'cp_1'=8,'cp_2'=2,'fs'=4] {'cp_0','cp_1','cp_2'}, dimensions={0} | all-to-all | bytes 4194304 | tf_op jit(solution)/shard_map/all_to_all | solution.py:79
  (103 shorter events, 27.9 us)
Async XLA Ops:
  7.2 76.3 %all-gather.7.cloned.1.call-start = ((), (), s32[]{:S(2)}) async-start(), calls=%async_computation.3 | async-start | bytes 2621440 | tf_op jit(solution)/shard_map/all_gather | solution.py:35
  42.6 62.6 %all-gather.9.cloned.1.call-start = ((), (), s32[]{:S(2)}) async-start(), calls=%async_computation.4 | async-start | bytes 6291456 | tf_op jit(solution)/shard_map/all_gather | solution.py:35
  83.5 24.4 %copy-start.14 = (bf16[1,256,4096]{2,1,0:T(8,128)(2,1)S(1)}, bf16[1,256,4096]{2,1,0:T(8,128)(2,1)}, u32[]{:S(2)}) copy-start(bf16[1,256,4096]{2,1,0:T(8,128)(2,1)} %param.10) | copy-start | bytes 6291460
  109.3 13.3 %collective-permute-start = (bf16[1,256,1024]{2,1,0:T(8,128)(2,1)S(1)}, bf16[1,256,1024]{2,1,0:T(8,128)(2,1)S(1)}, u32[]{:S(2)}, u32[]{:S(2)}) collective-permute-start(bf16[1,256,1024]{2,1,0:T(8,128)(2,1)S(1)} %maximum_bitcast_fusion), channel_id=1, source_target_pairs={{0,4},{4,8},{8,12},{12,16},{16,20},{20,24},{24,28},{28,32},{32,36}... | collective-permute-start | bytes 1572872 | tf_op jit(solution)/shard_map/ppermute | solution.py:49
  118.1 130.2 %all-to-all-start.1 = ((bf16[256,64,64]{0,1,2:T(8,128)(2,1)}), bf16[256,64,64]{0,1,2:T(8,128)(2,1)}, u32[]{:S(2)}, u32[]{:S(2)}) async-start(bf16[256,64,64]{0,1,2:T(8,128)(2,1)} %copy.124), calls=%async_computation.1 | async-start | bytes 4194304 | tf_op jit(solution)/shard_map/all_to_all | solution.py:203
  122.5 5.3 %copy-start.13 = (bf16[1,256,2048]{2,1,0:T(8,128)(2,1)S(1)}, bf16[1,256,2048]{2,1,0:T(8,128)(2,1)}, u32[]{:S(2)}) copy-start(bf16[1,256,2048]{2,1,0:T(8,128)(2,1)} %param.13) | copy-start | bytes 3145732
  122.5 5.5 %copy-start.15 = (bf16[1,256,1024]{2,1,0:T(8,128)(2,1)}, bf16[1,256,1024]{2,1,0:T(8,128)(2,1)S(1)}, u32[]{:S(2)}) copy-start(bf16[1,256,1024]{2,1,0:T(8,128)(2,1)S(1)} %collective-permute-done) | copy-start | bytes 1572868
  123.6 38.6 %collective-permute-start.1 = (bf16[2,256,1024]{2,1,0:T(8,128)(2,1)}, bf16[2,256,1024]{2,1,0:T(8,128)(2,1)}, u32[]{:S(2)}, u32[]{:S(2)}) collective-permute-start(bf16[2,256,1024]{2,1,0:T(8,128)(2,1)} %pad_maximum_fusion.3), channel_id=1, source_target_pairs={{0,8},{4,12},{8,16},{12,20},{16,24},{20,28},{24,32},{28,36},{32,40... | collective-permute-start | bytes 3145736 | tf_op jit(solution)/shard_map/ppermute | solution.py:49
  130.3 6.5 %copy-start.22 = (s32[1,256]{1,0:T(1,128)S(1)}, s32[1,256]{1,0:T(1,128)}, u32[]{:S(2)}) copy-start(s32[1,256]{1,0:T(1,128)} %param.14) | copy-start | bytes 3076
  132.3 29.9 %collective-permute-start.2 = (bf16[1,256,1024]{2,1,0:T(8,128)(2,1)S(1)}, bf16[1,256,1024]{2,1,0:T(8,128)(2,1)S(1)}, u32[]{:S(2)}, u32[]{:S(2)}) collective-permute-start(bf16[1,256,1024]{2,1,0:T(8,128)(2,1)S(1)} %maximum_bitcast_fusion), channel_id=1, source_target_pairs={{0,16},{4,20},{8,24},{12,28},{16,32},{20,36},{24,40},{28,44},{32,4... | collective-permute-start | bytes 1572872 | tf_op jit(solution)/shard_map/ppermute | solution.py:49
  165.7 5.2 %copy-start.16 = (bf16[1,256,2048]{1,2,0:T(8,128)(2,1)S(1)}, bf16[1,256,2048]{1,2,0:T(8,128)(2,1)}, u32[]{:S(2)}) copy-start(bf16[1,256,2048]{1,2,0:T(8,128)(2,1)} %copy.103) | copy-start | bytes 3145732
  186.3 4.0 %copy-start.7 = (bf16[5,256,1024]{2,1,0:T(8,128)(2,1)S(1)}, bf16[5,256,1024]{2,1,0:T(8,128)(2,1)}, u32[]{:S(2)}) copy-start(bf16[5,256,1024]{2,1,0:T(8,128)(2,1)} %rev.4) | copy-start | bytes 7864324
  190.8 4.6 %slice-start.2 = ((s8[5242880]{0:T(1024)(128)(4,1)}), s8[4194304]{0:T(1024)(128)(4,1)S(1)}, s32[]{:S(2)}) async-start(s8[5242880]{0:T(1024)(128)(4,1)} %bitcast.239), calls=%async_computation.7 | async-start | bytes 8388608
  190.8 4.6 %slice-start.3 = ((s8[5242880]{0:T(1024)(128)(4,1)}), s8[1048576]{0:T(1024)(128)(4,1)S(1)}, s32[]{:S(2)}) async-start(s8[5242880]{0:T(1024)(128)(4,1)} %bitcast.239), calls=%async_computation.8 | async-start | bytes 2097152
  194.8 2.2 copy-start
  195.4 6.0 %copy-start.8 = (f32[256,1,4,128]{0,3,2,1:T(8,128)}, f32[256,1,4,128]{0,3,2,1:T(8,128)S(1)}, u32[]{:S(2)}) copy-start(f32[256,1,4,128]{0,3,2,1:T(8,128)S(1)} %convolution_bitcast_fusion.7) | copy-start | bytes 1572868
  195.4 3.0 slice-start
  195.4 4.0 %slice-start.1 = ((s8[5242880]{0:T(1024)(128)(4,1)}), s8[1048576]{0:T(1024)(128)(4,1)S(1)}, s32[]{:S(2)}) async-start(s8[5242880]{0:T(1024)(128)(4,1)} %bitcast.237), calls=%async_computation.6 | async-start | bytes 2097152
  197.1 3.8 %copy-start.2 = (bf16[4,256,1280]{1,2,0:T(8,128)(2,1)}, bf16[4,256,1280]{1,2,0:T(8,128)(2,1)S(1)}, u32[]{:S(2)}) copy-start(bf16[4,256,1280]{1,2,0:T(8,128)(2,1)S(1)} %divide_convert_fusion.1) | copy-start | bytes 7864324
  197.6 3.8 %copy-start.10 = (f32[256,1,4,128]{0,3,2,1:T(8,128)}, f32[256,1,4,128]{0,3,2,1:T(8,128)S(1)}, u32[]{:S(2)}) copy-start(f32[256,1,4,128]{0,3,2,1:T(8,128)S(1)} %convolution_bitcast_fusion.6) | copy-start | bytes 1572868
  200.9 2.3 copy-start.4
  206.1 2.5 copy-start.6
  206.1 2.6 copy-start.9
  206.1 2.8 copy-start.11
  216.8 19.7 %collective-permute-start.3 = (bf16[2,256,512]{1,2,0:T(8,128)(2,1)S(1)}, bf16[2,256,512]{1,2,0:T(8,128)(2,1)S(1)}, u32[]{:S(2)}, u32[]{:S(2)}) collective-permute-start(bf16[2,256,512]{1,2,0:T(8,128)(2,1)S(1)} %pad_maximum_fusion.4), channel_id=1, source_target_pairs={{4,0},{8,4},{12,8},{16,12},{20,16},{24,20},{28,24},{32,28},{36,32}... | collective-permute-start | bytes 1572872 | tf_op jit(solution)/shard_map/ppermute | solution.py:49
  218.8 19.2 %collective-permute-start.5 = (bf16[1,256,512]{1,2,0:T(8,128)(2,1)S(1)}, bf16[1,256,512]{1,2,0:T(8,128)(2,1)S(1)}, u32[]{:S(2)}, u32[]{:S(2)}) collective-permute-start(bf16[1,256,512]{1,2,0:T(8,128)(2,1)S(1)} %get-tuple-element.11), channel_id=1, source_target_pairs={{16,0},{20,4},{24,8},{28,12},{32,16},{36,20},{40,24},{44,28},{48,3... | collective-permute-start | bytes 786440 | tf_op jit(solution)/shard_map/ppermute | solution.py:49
  236.6 11.4 %collective-permute-start.4 = (bf16[1,256,512]{1,2,0:T(8,128)(2,1)S(1)}, bf16[1,256,512]{1,2,0:T(8,128)(2,1)S(1)}, u32[]{:S(2)}, u32[]{:S(2)}) collective-permute-start(bf16[1,256,512]{1,2,0:T(8,128)(2,1)S(1)} %fusion.15), channel_id=1, source_target_pairs={{8,0},{12,4},{16,8},{20,12},{24,16},{28,20},{32,24},{36,28},{40,32... | collective-permute-start | bytes 786440 | tf_op jit(solution)/shard_map/ppermute | solution.py:49
  249.4 20.0 %all-to-all-start = ((bf16[4,256,512]{2,1,0:T(8,128)(2,1)}), bf16[4,256,512]{2,1,0:T(8,128)(2,1)S(1)}, u32[]{:S(2)}, u32[]{:S(2)}) async-start(bf16[4,256,512]{2,1,0:T(8,128)(2,1)} %broadcast_in_dim.58), calls=%async_computation | async-start | bytes 2097152 | tf_op jit(solution)/shard_map/all_to_all | solution.py:62
  275.0 69.1 %copy-start.18 = (bf16[16,512]{1,0:T(8,128)(2,1)S(1)}, bf16[16,512]{1,0:T(8,128)(2,1)}, u32[]{:S(2)}) copy-start(bf16[16,512]{1,0:T(8,128)(2,1)} %param.16) | copy-start | bytes 49156
  275.0 69.1 %copy-start.19 = (f32[16,512]{1,0:T(8,128)S(1)}, f32[16,512]{1,0:T(8,128)}, u32[]{:S(2)}) copy-start(f32[16,512]{1,0:T(8,128)} %param.18) | copy-start | bytes 98308
  275.0 69.1 %copy-start.20 = (f32[16,512]{1,0:T(8,128)S(1)}, f32[16,512]{1,0:T(8,128)}, u32[]{:S(2)}) copy-start(f32[16,512]{1,0:T(8,128)} %param.17) | copy-start | bytes 98308
  275.0 69.1 %copy-start.21 = (f32[16,512]{1,0:T(8,128)S(1)}, f32[16,512]{1,0:T(8,128)}, u32[]{:S(2)}) copy-start(f32[16,512]{1,0:T(8,128)} %param.19) | copy-start | bytes 98308
  (6 other events, 10.1 us)
Sparse Core Ops, SparseCore 0:
  42.8 40.6 all-gather.6
  85.3 19.9 all-gather.8
where the time goes:
time: 353 us; the launch traced here: 352 us
  waiting for transfers between devices  125 us (35%)
  blocking collectives  104 us (29%)
  matrix products  30.5 us (9%)
  local copies, waits for them, and re-layouts  29.6 us (8%)
  starting transfers between devices  25.4 us (7%)
  other arithmetic  22.1 us (6%)
  between operations  14.6 us (4%)
    all_to_all x1, blocking collectives, sum_at_owner(): lax.all_to_all(parts, axis, split_axis=0, concat_axis=0, tiled=True)  68.9 us
    all_gather x2, waiting for transfers between devices, gather_in_order(): parts = lax.all_gather(parts, axes[k])  62.5 us
    ppermute x6, waiting for transfers between devices, from_behind(): return lax.ppermute(block, axis, route)  50.9 us
    all_gather x2, blocking collectives, gather_in_order(): parts = lax.all_gather(parts, axes[k])  35.4 us
    sub x4, matrix products, block_attention(): weights = jnp.exp(scores - largest)  20.5 us
    ppermute x6, starting transfers between devices, from_behind(): return lax.ppermute(block, axis, route)  16.1 us
    all_to_all x1, waiting for transfers between devices, from_everyone(): lax.all_to_all(jnp.broadcast_to(shard[None], (count, *shard.shape)), axis...  11.6 us
    convert_element_type x4, other arithmetic, block_attention(): (weights / jnp.sum(weights, axis=-1, keepdims=True)).astype(jnp.bfloat16)  11 us
  transfers between devices with their start and end apart: 10, of which 6 were waited for; matrix products, arithmetic and copies ran while one was open for 19% of the time, Pallas kernels for 0%

commit v1 on v0

v1 whole, which is shorter than its diff:
```python
import math
from types import SimpleNamespace

import jax
import jax.numpy as jnp
from jax import lax
from jax.experimental import pallas as pl
from jax.experimental.pallas import tpu as pltpu
from jax.sharding import Mesh
from jax.sharding import PartitionSpec as P

HEAD = 128
KV = 4
WIN = 4
GROUP = 4
TOK = 256
SPAN = (WIN + 1) * TOK
NY, NZ, NX = 4, 8, 4
CP = ("cp_0", "cp_1", "cp_2")
CP_FS = ("cp_0", "cp_1", "cp_2", "fs")

NORM_EPS = 0.01
MOMENT_DECAY = 0.95
LEARN_RATE = 0.005
WEIGHT_DECAY = 0.1
ADAM_EPS = 1e-08
AVERAGE_MIX = 0.25
INTERP_BETA = 0.9
EXP2_SCALE = math.log2(math.e) / math.sqrt(HEAD)
MASKED = -1e30
FAR = 1 << 30

BF = jnp.bfloat16
F32 = jnp.float32
MESH = pl.DeviceIdType.MESH

BUFFERS = {
    "emb": ((8, TOK, 512), BF),
    "w": ((2, NY, NZ, 2, NX, 16, 256), BF),
    "q": ((TOK, 2048), BF),
    "kw": ((5, TOK, 512), BF),
    "vw": ((KV, 5, TOK, HEAD), BF),
    "cot": ((TOK, 2048), BF),
    "p": ((16, TOK, SPAN), BF),
    "s": ((TOK, SPAN), F32),
    "bias": ((TOK, SPAN), F32),
    "vacc": ((2, TOK, 256), F32),
    "att": ((16, TOK, HEAD), F32),
    "og": ((16, TOK, HEAD), BF),
    "dv": ((KV, 5, TOK, HEAD), F32),
    "r": ((KV, 3, TOK, HEAD), F32),
    "fo": ((KV, TOK, HEAD), BF),
    "fi": ((KV, TOK, HEAD), BF),
    "go": ((KV, TOK, HEAD), BF),
    "gi": ((KV, TOK, HEAD), BF),
    "vg": ((2, 8, TOK, 256), BF),
    "ex": ((8, TOK, 512), BF),
    "g": ((2, 4, 2, NX, 16, 256), F32),
    "x1": ((2, 2, 2, 2, 16, 256), F32),
    "tx": ((2, 2, 4, 2, 16, 256), F32),
    "x2": ((2, 2, 4, 2, 16, 256), F32),
    "t": ((2, 4, 2, 16, 256), F32),
    "rz": ((2, NZ, 16, 256), F32),
}
SEMAPHORES = {
    "ld": 16,
    "w1": 8,
    "w2": 6,
    "w3": 8,
    "wd": 10,
    "k": 4,
    "v": 16,
    "e": 8,
    "r": 8,
    "f": 4,
    "g": 4,
    "vg": 16,
    "vd": 16,
    "x": 8,
    "z": 16,
}


def kernel(need, doc, emb_h, q_h, k_h, cot_h, yw_h, out, *scratch):
    names = list(BUFFERS)
    b = SimpleNamespace(**dict(zip(names, scratch)))
    rest = scratch[len(names) :]
    snd = dict(zip(SEMAPHORES, rest[: len(SEMAPHORES)]))
    rcv = dict(zip(SEMAPHORES, rest[len(SEMAPHORES) :]))

    y, z = lax.axis_index("cp_0"), lax.axis_index("cp_1")
    c, x = lax.axis_index("cp_2"), lax.axis_index("fs")
    o = 1 - c
    zn, yn = lax.rem(z + 1, NZ), lax.rem(y + lax.div(z + 1, NZ), NY)
    zp, yp = lax.rem(z + NZ - 1, NZ), lax.rem(y + NY - 1 + lax.div(z + NZ - 1, NZ), NY)
    yup, ydn = lax.rem(y + 1, NY), lax.rem(y + NY - 1, NY)
    xup, xdn = lax.rem(x + 1, NX), lax.rem(x + NX - 1, NX)
    yop, xop = lax.rem(y + 2, NY), lax.rem(x + 2, NX)
    block = (y * NZ + z) * 2 + c

    def dev(cp_0=y, cp_1=z, cp_2=c, fs=x):
        return {"cp_0": cp_0, "cp_1": cp_1, "cp_2": cp_2, "fs": fs}

    sibling = dev(cp_2=o)
    following, preceding = dev(cp_0=yn, cp_1=zn), dev(cp_0=yp, cp_1=zp)

    started = []

    def copy(src, dst, kind, k, to):
        return pltpu.make_async_remote_copy(
            src_ref=src,
            dst_ref=dst,
            send_sem=snd[kind].at[k],
            recv_sem=rcv[kind].at[k],
            device_id=to,
            device_id_type=MESH,
        )

    def send(src, dst, kind, k, to):
        made = copy(src, dst, kind, k, to)
        made.start()
        started.append(made)

    def arrived(dst, kind, k):
        copy(dst, dst, kind, k, sibling).wait_recv()

    loads = {}

    def load(name, src, dst):
        loads[name] = pltpu.make_async_copy(src, dst, rcv["ld"].at[len(loads)])
        loads[name].start()

    mine = b.w.at[:, y, z, c, x]
    load("w0", yw_h.at[:, 0:256], b.w.at[0, y, z, c, x])
    load("w1", yw_h.at[:, 256:512], b.w.at[1, y, z, c, x])
    load("k", k_h, b.kw.at[0])
    load("q", q_h, b.q)
    for e in range(8):
        load("e%d" % e, emb_h.at[:, e * 512 : (e + 1) * 512], b.emb.at[e])
    load("cot", cot_h, b.cot)

    barrier = pltpu.get_barrier_semaphore()
    partners = [sibling, following, preceding]
    for d in range(1, NZ):
        for cc in (c, o):
            partners.append(dev(cp_1=lax.rem(z + d, NZ), cp_2=cc))
    for d in range(1, NY):
        for cc in (c, o):
            partners.append(dev(cp_0=lax.rem(y + d, NY), cp_2=cc))
        partners.append(dev(fs=lax.rem(x + d, NX)))
    for who in partners:
        pl.semaphore_signal(barrier, inc=1, device_id=who, device_id_type=MESH)
    pl.semaphore_wait(barrier, len(partners))

    loads["w0"].wait()
    loads["w1"].wait()
    for d in range(1, NZ):
        send(mine, mine, "w1", d, dev(cp_1=lax.rem(z + d, NZ)))
    loads["k"].wait()
    send(b.kw.at[0], b.kw.at[2], "k", 0, following)

    doc_t = jnp.transpose(jnp.broadcast_to(doc[...], (TOK, TOK)))
    row = lax.broadcasted_iota(jnp.int32, (TOK, TOK), 0) + block * TOK
    col = lax.broadcasted_iota(jnp.int32, (TOK, TOK), 1)
    for d in range(WIN + 1):
        listed = need[0, 0] == block - d
        for k in range(1, WIN + 1):
            listed = jnp.logical_or(listed, need[0, k] == block - d)
        shut = jnp.where(listed, 0, FAR)
        key_pos = col + (block - d) * TOK
        seen = jnp.logical_and(key_pos >= doc_t + shut, key_pos <= row)
        b.bias[:, d * TOK : (d + 1) * TOK] = jnp.where(seen, 0.0, MASKED)
    for kv in range(KV):
        b.r[kv, 2] = jnp.zeros((TOK, HEAD), F32)

    for d in range(1, NZ):
        arrived(mine, "w1", d)
    first, second = b.w.at[0, y, :, c, x], b.w.at[1, y, :, c, x]
    for d in range(1, 4):
        send(first, first, "w2", d - 1, dev(cp_0=lax.rem(y + d, NY)))
        send(second, second, "w2", d + 2, dev(fs=lax.rem(x + d, NX)))

    arrived(b.kw.at[2], "k", 0)
    send(b.kw.at[2], b.kw.at[4], "k", 1, following)
    send(b.kw.at[2 * c], b.kw.at[1], "k", 2, sibling)

    for d in range(6):
        arrived(first, "w2", d)

    def half_a(xx):
        return b.w.at[0, :, :, c, xx]

    def half_b(yy):
        return b.w.at[1, yy, :, c, :]

    def relay_a(xx, s):
        return b.w.at[0, :, 4 * s : 4 * s + 4, c, xx]

    def relay_b(yy, s):
        return b.w.at[1, yy, 4 * s : 4 * s + 4, c, :]

    send(half_a(x), half_a(x), "w3", 0, dev(fs=xup))
    send(half_a(x), half_a(x), "w3", 1, dev(fs=xdn))
    send(half_b(y), half_b(y), "w3", 2, dev(cp_0=yup))
    send(half_b(y), half_b(y), "w3", 3, dev(cp_0=ydn))
    send(half_a(x), half_a(x), "wd", 0, sibling)
    send(half_b(y), half_b(y), "wd", 1, sibling)

    arrived(b.kw.at[4], "k", 1)
    send(b.kw.at[2 + 2 * c], b.kw.at[3], "k", 3, sibling)
    arrived(b.kw.at[1], "k", 2)
    arrived(b.kw.at[3], "k", 3)
    loads["q"].wait()

    def head_probs(hd, carry):
        lanes = pl.ds(pl.multiple_of(hd * HEAD, HEAD), HEAD)
        key_lanes = pl.ds(pl.multiple_of(lax.div(hd, GROUP) * HEAD, HEAD), HEAD)
        keys = b.kw[:, :, key_lanes].reshape(SPAN, HEAD)
        b.s[...] = lax.dot_general(
            b.q[:, lanes], keys, (((1,), (1,)), ((), ())), preferred_element_type=F32
        )
        for n in range(8):
            rows = slice(n * 32, n * 32 + 32)
            score = b.s[rows, :] + b.bias[rows, :]
            largest = jnp.max(score, axis=-1, keepdims=True)
            weight = jnp.exp2((score - largest) * EXP2_SCALE)
            total = jnp.sum(weight, axis=-1, keepdims=True)
            b.p[hd, rows, :] = (weight * (1.0 / total)).astype(BF)
        return carry

    lax.fori_loop(0, 6, head_probs, 0)

    arrived(half_a(x), "w3", 0)
    send(relay_a(xdn, 0), relay_a(xdn, 0), "w3", 4, dev(fs=xup))
    send(half_a(xdn), half_a(xdn), "wd", 2, sibling)
    arrived(half_a(x), "w3", 1)
    send(relay_a(xup, 1), relay_a(xup, 1), "w3", 5, dev(fs=xdn))
    send(half_a(xup), half_a(xup), "wd", 3, sibling)
    arrived(half_b(y), "w3", 2)
    send(relay_b(ydn, 0), relay_b(ydn, 0), "w3", 6, dev(cp_0=yup))
    send(half_b(ydn), half_b(ydn), "wd", 4, sibling)
    arrived(half_b(y), "w3", 3)
    send(relay_b(yup, 1), relay_b(yup, 1), "w3", 7, dev(cp_0=ydn))
    send(half_b(yup), half_b(yup), "wd", 5, sibling)

    for e in range(8):
        loads["e%d" % e].wait()
    own = y * 2 + c
    kept = pltpu.make_async_copy(b.emb.at[own], b.ex.at[own], rcv["ld"].at[14])
    kept.start()
    send(b.emb.at[y * 2 + o], b.ex.at[own], "e", 0, sibling)
    for d in range(1, NY):
        yt = lax.rem(y + d, NY)
        for k, cc in enumerate((c, o)):
            send(b.emb.at[yt * 2 + cc], b.ex.at[own], "e", d * 2 + k, dev(cp_0=yt, cp_2=cc))

    lax.fori_loop(6, 16, head_probs, 0)

    for s in range(2):
        arrived(relay_a(x, s), "w3", 4 + s)
        send(relay_a(xop, s), relay_a(xop, s), "wd", 6 + s, sibling)
    for s in range(2):
        arrived(relay_b(y, s), "w3", 6 + s)
        send(relay_b(yop, s), relay_b(yop, s), "wd", 8 + s, sibling)
    for k in (0, 2, 3):
        arrived(half_a(x), "wd", k)
    for k in (1, 4, 5):
        arrived(half_b(y), "wd", k)
    for s in range(2):
        arrived(relay_a(x, s), "wd", 6 + s)
        arrived(relay_b(y, s), "wd", 8 + s)

    for h in range(2):
        b.vacc[h] = jnp.zeros((TOK, 256), F32)

        def add_chunk(e, carry):
            yy, low = lax.div(e, 2), 4 * lax.rem(e, 2)
            rows = b.w[h, yy, pl.ds(low, 4)].reshape(512, 256)
            b.vacc[h] += jnp.dot(b.emb[e], rows, preferred_element_type=F32)
            return carry

        lax.fori_loop(0, 8, add_chunk, 0)
        for k in range(2):
            kv = 2 * h + k
            b.vw[kv, 0] = b.vacc[h, :, k * HEAD : (k + 1) * HEAD].astype(BF)
            send(b.vw.at[kv, 0], b.vw.at[kv, 2], "v", kv, following)

    for kv in range(KV):
        arrived(b.vw.at[kv, 2], "v", kv)
        send(b.vw.at[kv, 2], b.vw.at[kv, 4], "v", 4 + kv, following)
        send(b.vw.at[kv, 2 * c], b.vw.at[kv, 1], "v", 8 + kv, sibling)

    def attend(kv):
        arrived(b.vw.at[kv, 1], "v", 8 + kv)
        arrived(b.vw.at[kv, 3], "v", 12 + kv)

        def one(k, carry):
            hd = kv * GROUP + k
            b.att[hd] = jnp.dot(
                b.p[hd], b.vw[kv].reshape(SPAN, HEAD), preferred_element_type=F32
            )
            return carry

        lax.fori_loop(0, GROUP, one, 0)

    for kv in range(KV):
        arrived(b.vw.at[kv, 4], "v", 4 + kv)
        send(b.vw.at[kv, 2 + 2 * c], b.vw.at[kv, 3], "v", 12 + kv, sibling)
        if kv:
            attend(kv - 1)
    attend(KV - 1)

    loads["cot"].wait()
    token_total = TOK * NY * NZ * 2 * NX

    def norm_rows(n, carry):
        rows = pl.ds(pl.multiple_of(n * 32, 32), 32)
        squares = jnp.zeros((32, HEAD), F32)
        crossed = jnp.zeros((32, HEAD), F32)
        for hd in range(16):
            a = b.att[hd, rows, :]
            squares += a * a
            crossed += a * b.cot[rows, hd * HEAD : (hd + 1) * HEAD].astype(F32)
        mean = jnp.sum(squares, axis=-1, keepdims=True) / 2048.0 + NORM_EPS
        inv = 1.0 / jnp.sqrt(mean)
        inner = jnp.sum(crossed, axis=-1, keepdims=True) / (2048.0 * token_total) * inv
        factor = inner * inv
        for hd in range(16):
            up = b.cot[rows, hd * HEAD : (hd + 1) * HEAD].astype(F32) / token_total
            b.og[hd, rows, :] = ((up - b.att[hd, rows, :] * factor) * inv).astype(BF)
        return carry

    lax.fori_loop(0, 8, norm_rows, 0)

    def grads(kv):
        def one(d, carry):
            lanes = pl.ds(pl.multiple_of(d * TOK, TOK), TOK)
            part = b.p[kv * GROUP : kv * GROUP + GROUP, :, lanes].reshape(GROUP * TOK, TOK)
            up = b.og[kv * GROUP : kv * GROUP + GROUP].reshape(GROUP * TOK, HEAD)
            b.dv[kv, d] = lax.dot_general(
                part, up, (((0,), (0,)), ((), ())), preferred_element_type=F32
            )
            return carry

        lax.fori_loop(0, WIN + 1, one, 0)
        send(b.dv.at[kv, 1], b.r.at[kv, 0], "r", 2 * kv, sibling)
        send(b.dv.at[kv, 3], b.r.at[kv, 1], "r", 2 * kv + 1, sibling)

    def leave_far(kv):
        arrived(b.r.at[kv, 0], "r", 2 * kv)
        arrived(b.r.at[kv, 1], "r", 2 * kv + 1)
        b.fo[kv] = (b.dv[kv, 4] + b.r[kv, 2 - c]).astype(BF)
        send(b.fo.at[kv], b.fi.at[kv], "f", kv, preceding)

    def leave_near(kv):
        arrived(b.fi.at[kv], "f", kv)
        b.go[kv] = (b.dv[kv, 2] + b.r[kv, 1 - c] + b.fi[kv].astype(F32)).astype(BF)
        send(b.go.at[kv], b.gi.at[kv], "g", kv, preceding)

    def vg_at(kv, yy, cc, rows=slice(None)):
        lanes = slice((kv % 2) * HEAD, (kv % 2) * HEAD + HEAD)
        return b.vg.at[kv // 2, yy * 2 + cc, rows, lanes]

    upper, lower = slice(0, 128), slice(128, 256)

    def settle(kv):
        arrived(b.gi.at[kv], "g", kv)
        total = b.dv[kv, 0] + b.r[kv, 2 * c] + b.gi[kv].astype(F32)
        b.vg[kv // 2, own, :, (kv % 2) * HEAD : (kv % 2) * HEAD + HEAD] = total.astype(BF)
        here = vg_at(kv, y, c)
        send(here, here, "vg", 4 * kv, dev(cp_0=yup))
        send(here, here, "vg", 4 * kv + 1, dev(cp_0=ydn))
        send(here, here, "vd", 4 * kv, sibling)

    def relay(kv):
        arrived(vg_at(kv, y, c), "vg", 4 * kv)
        part = vg_at(kv, ydn, c, upper)
        send(part, part, "vg", 4 * kv + 2, dev(cp_0=yup))
        send(vg_at(kv, ydn, c), vg_at(kv, ydn, c), "vd", 4 * kv + 1, sibling)
        arrived(vg_at(kv, y, c), "vg", 4 * kv + 1)
        part = vg_at(kv, yup, c, lower)
        send(part, part, "vg", 4 * kv + 3, dev(cp_0=ydn))
        send(vg_at(kv, yup, c), vg_at(kv, yup, c), "vd", 4 * kv + 2, sibling)

    def collect(kv):
        arrived(vg_at(kv, y, c, upper), "vg", 4 * kv + 2)
        arrived(vg_at(kv, y, c, lower), "vg", 4 * kv + 3)
        send(vg_at(kv, yop, c), vg_at(kv, yop, c), "vd", 4 * kv + 3, sibling)

    def complete(kv):
        for k in range(4):
            arrived(vg_at(kv, y, c), "vd", 4 * kv + k)

    grads(0)
    grads(1)
    leave_far(0)
    grads(2)
    leave_far(1)
    grads(3)
    leave_far(2)
    leave_far(3)
    for kv in range(KV):
        leave_near(kv)
    settle(0)
    settle(1)
    relay(0)
    settle(2)
    relay(1)
    collect(0)

    kept.wait()
    arrived(b.ex.at[0], "e", 0)
    for d in range(2, 8):
        arrived(b.ex.at[0], "e", d)

    settle(3)
    relay(2)
    collect(1)
    complete(0)
    complete(1)

    def product(h):
        grad = lax.dot_general(
            b.ex[...].reshape(8 * TOK, 512),
            b.vg[h].reshape(8 * TOK, 256),
            (((0,), (0,)), ((), ())),
            preferred_element_type=F32,
        )
        b.g[h] = grad.reshape(4, 2, NX, 16, 256)
        send(b.g.at[h, 0:2, :, xop], b.x1.at[h, 0], "x", 4 * h, dev(fs=xup))
        send(b.g.at[h, 2:4, :, xop], b.x1.at[h, 1], "x", 4 * h + 1, dev(fs=xdn))

    def across(h):
        arrived(b.x1.at[h, 0], "x", 4 * h)
        b.tx[h, 0, 0:2] = b.g[h, 0:2, :, xup] + b.x1[h, 0]
        b.tx[h, 0, 2:4] = b.g[h, 2:4, :, xup]
        send(b.tx.at[h, 0], b.x2.at[h, 0], "x", 4 * h + 2, dev(fs=xup))
        arrived(b.x1.at[h, 1], "x", 4 * h + 1)
        b.tx[h, 1, 0:2] = b.g[h, 0:2, :, xdn]
        b.tx[h, 1, 2:4] = b.g[h, 2:4, :, xdn] + b.x1[h, 1]
        send(b.tx.at[h, 1], b.x2.at[h, 1], "x", 4 * h + 3, dev(fs=xdn))

    def along(h):
        arrived(b.x2.at[h, 0], "x", 4 * h + 2)
        arrived(b.x2.at[h, 1], "x", 4 * h + 3)
        b.t[h] = b.g[h, :, :, x] + b.x2[h, 0] + b.x2[h, 1]
        for k in range(4):
            for cc in range(2):
                zt = 4 * c + k
                stays = jnp.logical_and(zt == z, c == cc)

                @pl.when(stays)
                def _():
                    b.rz[h, z] = b.t[h, k, cc]

                @pl.when(jnp.logical_not(stays))
                def _():
                    pltpu.make_async_remote_copy(
                        src_ref=b.t.at[h, k, cc],
                        dst_ref=b.rz.at[h, z],
                        send_sem=snd["z"].at[8 * h + 2 * k + cc],
                        recv_sem=rcv["z"].at[8 * h + z],
                        device_id=dev(cp_1=zt, cp_2=cc),
                        device_id_type=MESH,
                    ).start()

    def finish(h):
        for zs in range(NZ):
            stays = jnp.logical_and(zs == z, lax.div(z, 4) == c)

            @pl.when(jnp.logical_not(stays))
            def _():
                arrived(b.rz.at[h, 0], "z", 8 * h + zs)

        total = b.rz[h, 0]
        for zs in range(1, NZ):
            total = total + b.rz[h, zs]
        out[:, h * 256 : (h + 1) * 256] = total

    product(0)
    relay(3)
    collect(2)
    across(0)
    collect(3)
    complete(2)
    complete(3)
    product(1)
    along(0)
    across(1)
    along(1)
    finish(0)
    finish(1)

    for made in started:
        made.wait_send()
    for h in range(2):
        for k in range(4):
            for cc in range(2):
                stays = jnp.logical_and(4 * c + k == z, c == cc)

                @pl.when(jnp.logical_not(stays))
                def _():
                    copy(b.t.at[h, k, cc], b.rz.at[h, 0], "z", 8 * h + 2 * k + cc, sibling).wait_send()


def weight_gradient(need_ids, doc_start, embeds, queries, key_heads, cotangent, y_weight):
    any_space = pl.BlockSpec(memory_space=pl.ANY)
    vmem = pl.BlockSpec(memory_space=pltpu.VMEM)
    semaphores = [pltpu.SemaphoreType.DMA((n,)) for n in SEMAPHORES.values()]
    return pl.pallas_call(
        kernel,
        out_shape=jax.ShapeDtypeStruct((16, 512), F32),
        in_specs=[pl.BlockSpec(memory_space=pltpu.SMEM), vmem] + [any_space] * 5,
        out_specs=vmem,
        scratch_shapes=[pltpu.VMEM(shape, kind) for shape, kind in BUFFERS.values()]
        + semaphores
        + semaphores,
        compiler_params=pltpu.CompilerParams(
            collective_id=0, has_side_effects=True, vmem_limit_bytes=58 << 20
        ),
    )(need_ids, doc_start, embeds, queries, key_heads, cotangent, y_weight)


def on_device(
    embeds,
    queries,
    key_heads,
    cotangent,
    doc_start,
    need_ids,
    y_weight,
    z_weight,
    x_weight,
    second_moment,
):
    gradient = weight_gradient(
        need_ids[0], doc_start, embeds[0], queries[0], key_heads[0], cotangent[0], y_weight
    )
    moment_next = MOMENT_DECAY * second_moment + (1.0 - MOMENT_DECAY) * gradient * gradient
    z_next = z_weight - LEARN_RATE * (
        gradient / (jnp.sqrt(moment_next) + ADAM_EPS) + WEIGHT_DECAY * y_weight.astype(jnp.float32)
    )
    x_next = (1.0 - AVERAGE_MIX) * x_weight + AVERAGE_MIX * z_next
    y_next = ((1.0 - INTERP_BETA) * z_next + INTERP_BETA * x_next).astype(jnp.bfloat16)
    return (z_next, x_next, moment_next, y_next)


def solution(mesh):
    finer = Mesh(mesh.devices.reshape(NY, NZ, 2, mesh.shape["fs"]), CP_FS)
    return jax.shard_map(
        on_device,
        mesh=finer,
        in_specs=(
            P("fs", CP, None),
            P("fs", CP, None),
            P("fs", CP, None),
            P("fs", CP, None),
            P("fs", CP),
            P("fs", CP, None),
            P(CP_FS, None),
            P(CP_FS, None),
            P(CP_FS, None),
            P(CP_FS, None),
        ),
        out_specs=(P(CP_FS, None), P(CP_FS, None), P(CP_FS, None), P(CP_FS, None)),
        check_vma=False,
    )
```

time: 353 us -> 122 us (0.35)
  waiting for transfers between devices: 125 us -> 0 us
  Pallas kernels: 0 us -> 120 us
  blocking collectives: 104 us -> 0 us
  matrix products: 30.5 us -> 0 us
  local copies, waits for them, and re-layouts: 29.6 us -> 0.02 us
  starting transfers between devices: 25.4 us -> 0 us
  other arithmetic: 22.1 us -> 1.42 us
  between operations: 14.6 us -> 0.71 us
    pallas_call x0 -> x1, Pallas kernels: none -> 120 us  [weight_gradient(): pl.pallas_call(kernel, out_shape=jax.ShapeDtypeStruct((16, 512), F32), in...]
    all_to_all x1 -> x0, blocking collectives: 68.9 us -> none  [sum_at_owner(): lax.all_to_all(parts, axis, split_axis=0, concat_axis=0, tiled=True)]
    all_gather x2 -> x0, waiting for transfers between devices: 62.5 us -> none  [gather_in_order(): parts = lax.all_gather(parts, axes[k])]
    ppermute x6 -> x0, waiting for transfers between devices: 50.9 us -> none  [from_behind(): return lax.ppermute(block, axis, route)]
    all_gather x2 -> x0, blocking collectives: 35.4 us -> none  [gather_in_order(): parts = lax.all_gather(parts, axes[k])]
    sub x4 -> x0, matrix products: 20.5 us -> none  [block_attention(): weights = jnp.exp(scores - largest)]
    ppermute x6 -> x0, starting transfers between devices: 16.1 us -> none  [from_behind(): return lax.ppermute(block, axis, route)]
    convert_element_type x6 -> x0, other arithmetic: 12.6 us -> none  [the longest x4 11 us: block_attention(): (weights / jnp.sum(weights, axis=-1, keepdims=True)).astype(jnp.bfloat16)]
  transfers between devices with their start and end apart: 10 -> 0, of which waited for: 6 -> 0; matrix products, arithmetic and copies ran while one was open for 19% -> 0% of each run, Pallas kernels for 0% -> 0%
where the time goes in v1:
time: 122 us
  Pallas kernels  120 us (98%)
  other arithmetic  1.42 us (1%)
    pallas_call x1, Pallas kernels, weight_gradient(): pl.pallas_call(kernel, out_shape=jax.ShapeDtypeStruct((16, 512), F32), in...  120 us

profile of v1, /device:TPU:1, one launch (start us, length us, event | category | flops | bytes accessed | tf_op | source)
XLA Modules:
  0.0 122.1 jit_solution(14331966438575310295)
XLA Ops:
  0.6 0.0 copy-start
  0.6 0.0 copy-start.1
  0.7 0.0 copy-start.2
  0.7 0.0 copy-start.3
  0.7 120.0 %shard_map.129 = f32[16,512]{1,0:T(8,128)} custom-call(s32[1,5]{1,0:T(1,128)} %bitcast.9, s32[1,256]{1,0:T(1,128)} %doc.1, bf16[256,4096]{1,0:T(8,128)(2,1)} %bitcast.5, bf16[256,2048]{1,0:T(8,128)(2,1)} %bitcast.6, bf16[256,512]{1,0:T(8,128)(2,1)} %bitcast.8, bf16[256,2048]{1,0:T(8,128)(2,1)} %bitcast.7, bf16[16,512]{1,0:T(8,128)(2,1)} %yw_h.1), custom_call_target="tpu_custom_call" | custom-call | tf_op jit(solution)/shard_map/pallas_call | solution.py:510
  120.7 0.0 copy-done
  120.7 0.0 copy-done.1
  120.7 0.0 copy-done.2
  120.7 0.0 copy-done.3
  120.7 1.4 %add_convert_fusion = (bf16[16,512]{1,0:T(8,128)(2,1)}, f32[16,512]{1,0:T(8,128)}, f32[16,512]{1,0:T(8,128)}, f32[16,512]{1,0:T(8,128)}) fusion(f32[16,512]{1,0:T(8,128)S(1)} %copy-done.1, f32[16,512]{1,0:T(8,128)S(1)} %copy-done.2, bf16[16,512]{1,0:T(8,128)(2,1)S(1)} %copy-done, f32[16,512]{1,0:T(8,128)} %shard_map.129, f32[16,512]{1,0:T(8,128)S(1)} %copy-done.3), kind=kLoop, calls=%fused_computation.2 | loop fusion | flops 147456 | bytes 262144 | tf_op jit(solution)/shard_map/convert_element_type | solution.py:544
Async XLA Ops:
  0.6 120.0 %copy-start = (bf16[16,512]{1,0:T(8,128)(2,1)S(1)}, bf16[16,512]{1,0:T(8,128)(2,1)}, u32[]{:S(2)}) copy-start(bf16[16,512]{1,0:T(8,128)(2,1)} %yw_h.1) | copy-start | bytes 49156
  0.6 120.0 %copy-start.1 = (f32[16,512]{1,0:T(8,128)S(1)}, f32[16,512]{1,0:T(8,128)}, u32[]{:S(2)}) copy-start(f32[16,512]{1,0:T(8,128)} %param.18) | copy-start | bytes 98308
  0.7 120.0 %copy-start.2 = (f32[16,512]{1,0:T(8,128)S(1)}, f32[16,512]{1,0:T(8,128)}, u32[]{:S(2)}) copy-start(f32[16,512]{1,0:T(8,128)} %param.17) | copy-start | bytes 98308
  0.7 120.0 %copy-start.3 = (f32[16,512]{1,0:T(8,128)S(1)}, f32[16,512]{1,0:T(8,128)}, u32[]{:S(2)}) copy-start(f32[16,512]{1,0:T(8,128)} %param.19) | copy-start | bytes 98308

commit v2 on v1

--- a/solution.py
+++ b/solution.py
@@ -35,7 +35,7 @@
 MESH = pl.DeviceIdType.MESH
 
 BUFFERS = {
-    "emb": ((8, TOK, 512), BF),
+    "emb": ((TOK, 4096), BF),
     "w": ((2, NY, NZ, 2, NX, 16, 256), BF),
     "q": ((TOK, 2048), BF),
     "kw": ((5, TOK, 512), BF),
@@ -44,7 +44,6 @@
     "p": ((16, TOK, SPAN), BF),
     "s": ((TOK, SPAN), F32),
     "bias": ((TOK, SPAN), F32),
-    "vacc": ((2, TOK, 256), F32),
     "att": ((16, TOK, HEAD), F32),
     "og": ((16, TOK, HEAD), BF),
     "dv": ((KV, 5, TOK, HEAD), F32),
@@ -54,6 +53,7 @@
     "go": ((KV, TOK, HEAD), BF),
     "gi": ((KV, TOK, HEAD), BF),
     "vg": ((2, 8, TOK, 256), BF),
+    "er": ((2, 2, 128, 512), BF),
     "ex": ((8, TOK, 512), BF),
     "g": ((2, 4, 2, NX, 16, 256), F32),
     "x1": ((2, 2, 2, 2, 16, 256), F32),
@@ -70,7 +70,7 @@
     "wd": 10,
     "k": 4,
     "v": 16,
-    "e": 8,
+    "e": 16,
     "r": 8,
     "f": 4,
     "g": 4,
@@ -135,8 +135,7 @@
     load("w1", yw_h.at[:, 256:512], b.w.at[1, y, z, c, x])
     load("k", k_h, b.kw.at[0])
     load("q", q_h, b.q)
-    for e in range(8):
-        load("e%d" % e, emb_h.at[:, e * 512 : (e + 1) * 512], b.emb.at[e])
+    load("emb", emb_h, b.emb)
     load("cot", cot_h, b.cot)
 
     barrier = pltpu.get_barrier_semaphore()
@@ -180,10 +179,6 @@
         send(first, first, "w2", d - 1, dev(cp_0=lax.rem(y + d, NY)))
         send(second, second, "w2", d + 2, dev(fs=lax.rem(x + d, NX)))
 
-    arrived(b.kw.at[2], "k", 0)
-    send(b.kw.at[2], b.kw.at[4], "k", 1, following)
-    send(b.kw.at[2 * c], b.kw.at[1], "k", 2, sibling)
-
     for d in range(6):
         arrived(first, "w2", d)
 
@@ -203,11 +198,29 @@
     send(half_a(x), half_a(x), "w3", 1, dev(fs=xdn))
     send(half_b(y), half_b(y), "w3", 2, dev(cp_0=yup))
     send(half_b(y), half_b(y), "w3", 3, dev(cp_0=ydn))
+
+    arrived(b.kw.at[2], "k", 0)
+    send(b.kw.at[2], b.kw.at[4], "k", 1, following)
+    send(b.kw.at[2 * c], b.kw.at[1], "k", 2, sibling)
     send(half_a(x), half_a(x), "wd", 0, sibling)
     send(half_b(y), half_b(y), "wd", 1, sibling)
 
     arrived(b.kw.at[4], "k", 1)
     send(b.kw.at[2 + 2 * c], b.kw.at[3], "k", 3, sibling)
+
+    arrived(half_a(x), "w3", 0)
+    send(relay_a(xdn, 0), relay_a(xdn, 0), "w3", 4, dev(fs=xup))
+    arrived(half_a(x), "w3", 1)
+    send(relay_a(xup, 1), relay_a(xup, 1), "w3", 5, dev(fs=xdn))
+    arrived(half_b(y), "w3", 2)
+    send(relay_b(ydn, 0), relay_b(ydn, 0), "w3", 6, dev(cp_0=yup))
+    arrived(half_b(y), "w3", 3)
+    send(relay_b(yup, 1), relay_b(yup, 1), "w3", 7, dev(cp_0=ydn))
+    send(half_a(xdn), half_a(xdn), "wd", 2, sibling)
+    send(half_a(xup), half_a(xup), "wd", 3, sibling)
+    send(half_b(ydn), half_b(ydn), "wd", 4, sibling)
+    send(half_b(yup), half_b(yup), "wd", 5, sibling)
+
     arrived(b.kw.at[1], "k", 2)
     arrived(b.kw.at[3], "k", 3)
     loads["q"].wait()
@@ -230,38 +243,13 @@
 
     lax.fori_loop(0, 6, head_probs, 0)
 
-    arrived(half_a(x), "w3", 0)
-    send(relay_a(xdn, 0), relay_a(xdn, 0), "w3", 4, dev(fs=xup))
-    send(half_a(xdn), half_a(xdn), "wd", 2, sibling)
-    arrived(half_a(x), "w3", 1)
-    send(relay_a(xup, 1), relay_a(xup, 1), "w3", 5, dev(fs=xdn))
-    send(half_a(xup), half_a(xup), "wd", 3, sibling)
-    arrived(half_b(y), "w3", 2)
-    send(relay_b(ydn, 0), relay_b(ydn, 0), "w3", 6, dev(cp_0=yup))
-    send(half_b(ydn), half_b(ydn), "wd", 4, sibling)
-    arrived(half_b(y), "w3", 3)
-    send(relay_b(yup, 1), relay_b(yup, 1), "w3", 7, dev(cp_0=ydn))
-    send(half_b(yup), half_b(yup), "wd", 5, sibling)
-
-    for e in range(8):
-        loads["e%d" % e].wait()
-    own = y * 2 + c
-    kept = pltpu.make_async_copy(b.emb.at[own], b.ex.at[own], rcv["ld"].at[14])
-    kept.start()
-    send(b.emb.at[y * 2 + o], b.ex.at[own], "e", 0, sibling)
-    for d in range(1, NY):
-        yt = lax.rem(y + d, NY)
-        for k, cc in enumerate((c, o)):
-            send(b.emb.at[yt * 2 + cc], b.ex.at[own], "e", d * 2 + k, dev(cp_0=yt, cp_2=cc))
-
-    lax.fori_loop(6, 16, head_probs, 0)
-
     for s in range(2):
         arrived(relay_a(x, s), "w3", 4 + s)
         send(relay_a(xop, s), relay_a(xop, s), "wd", 6 + s, sibling)
     for s in range(2):
         arrived(relay_b(y, s), "w3", 6 + s)
         send(relay_b(yop, s), relay_b(yop, s), "wd", 8 + s, sibling)
+    lax.fori_loop(6, 8, head_probs, 0)
     for k in (0, 2, 3):
         arrived(half_a(x), "wd", k)
     for k in (1, 4, 5):
@@ -270,45 +258,92 @@
         arrived(relay_a(x, s), "wd", 6 + s)
         arrived(relay_b(y, s), "wd", 8 + s)
 
+    loads["emb"].wait()
     for h in range(2):
-        b.vacc[h] = jnp.zeros((TOK, 256), F32)
-
-        def add_chunk(e, carry):
-            yy, low = lax.div(e, 2), 4 * lax.rem(e, 2)
-            rows = b.w[h, yy, pl.ds(low, 4)].reshape(512, 256)
-            b.vacc[h] += jnp.dot(b.emb[e], rows, preferred_element_type=F32)
-            return carry
-
-        lax.fori_loop(0, 8, add_chunk, 0)
+        made = jnp.dot(b.emb[...], b.w[h].reshape(4096, 256), preferred_element_type=F32)
         for k in range(2):
             kv = 2 * h + k
-            b.vw[kv, 0] = b.vacc[h, :, k * HEAD : (k + 1) * HEAD].astype(BF)
+            b.vw[kv, 0] = made[:, k * HEAD : (k + 1) * HEAD].astype(BF)
             send(b.vw.at[kv, 0], b.vw.at[kv, 2], "v", kv, following)
 
+    def emb_at(yy, cc):
+        return b.emb.at[:, pl.ds(pl.multiple_of((yy * 2 + cc) * 512, 512), 512)]
+
+    def emb_part(yy, cc, s):
+        return b.emb.at[
+            128 * s : 128 * s + 128, pl.ds(pl.multiple_of((yy * 2 + cc) * 512, 512), 512)
+        ]
+
+    own = y * 2 + c
+    kept = pltpu.make_async_copy(emb_at(y, c), b.ex.at[own], rcv["ld"].at[14])
+    kept.start()
+    send(emb_at(y, o), b.ex.at[own], "e", 0, sibling)
+    for s, yt in enumerate((yup, ydn)):
+        for k, cc in enumerate((c, o)):
+            send(emb_part(yop, cc, s), b.er.at[s, k], "e", 8 + 2 * s + k, dev(cp_0=yt))
+    for s, yt in enumerate((yup, ydn)):
+        for k, cc in enumerate((c, o)):
+            send(emb_at(yt, cc), b.ex.at[own], "e", 2 + 2 * s + k, dev(cp_0=yt, cp_2=cc))
+
+    def pass_embeds():
+        for s, (yt, yf) in enumerate(((yup, ydn), (ydn, yup))):
+            for k, cc in enumerate((c, o)):
+                arrived(b.er.at[s, k], "e", 8 + 2 * s + k)
+                send(
+                    b.er.at[s, k],
+                    b.ex.at[yf * 2 + c, 128 * s : 128 * s + 128],
+                    "e",
+                    12 + 2 * s + k,
+                    dev(cp_0=yt, cp_2=cc),
+                )
+
+    lax.fori_loop(8, 12, head_probs, 0)
     for kv in range(KV):
         arrived(b.vw.at[kv, 2], "v", kv)
         send(b.vw.at[kv, 2], b.vw.at[kv, 4], "v", 4 + kv, following)
         send(b.vw.at[kv, 2 * c], b.vw.at[kv, 1], "v", 8 + kv, sibling)
-
-    def attend(kv):
+    lax.fori_loop(12, 16, head_probs, 0)
+    near, far = 3 * TOK, 2 * TOK
+
+    def attend_near(kv):
         arrived(b.vw.at[kv, 1], "v", 8 + kv)
-        arrived(b.vw.at[kv, 3], "v", 12 + kv)
 
         def one(k, carry):
             hd = kv * GROUP + k
-            b.att[hd] = jnp.dot(
-                b.p[hd], b.vw[kv].reshape(SPAN, HEAD), preferred_element_type=F32
-            )
+            values = b.vw[kv, 0:3].reshape(near, HEAD)
+            b.att[hd] = jnp.dot(b.p[hd, :, 0:near], values, preferred_element_type=F32)
             return carry
 
         lax.fori_loop(0, GROUP, one, 0)
 
-    for kv in range(KV):
+    def attend_far(kv):
+        arrived(b.vw.at[kv, 3], "v", 12 + kv)
+
+        def one(k, carry):
+            hd = kv * GROUP + k
+            values = b.vw[kv, 3:5].reshape(far, HEAD)
+            b.att[hd] += jnp.dot(b.p[hd, :, near:SPAN], values, preferred_element_type=F32)
+            return carry
+
+        lax.fori_loop(0, GROUP, one, 0)
+
+    def pass_values(kv):
         arrived(b.vw.at[kv, 4], "v", 4 + kv)
         send(b.vw.at[kv, 2 + 2 * c], b.vw.at[kv, 3], "v", 12 + kv, sibling)
-        if kv:
-            attend(kv - 1)
-    attend(KV - 1)
+
+    attend_near(0)
+    attend_near(1)
+    pass_values(0)
+    attend_near(2)
+    attend_near(3)
+    pass_values(1)
+    attend_far(0)
+    pass_values(2)
+    attend_far(1)
+    pass_embeds()
+    pass_values(3)
+    attend_far(2)
+    attend_far(3)
 
     loads["cot"].wait()
     token_total = TOK * NY * NZ * 2 * NX
@@ -332,7 +367,7 @@
 
     lax.fori_loop(0, 8, norm_rows, 0)
 
-    def grads(kv):
+    def grads(kv, low, high):
         def one(d, carry):
             lanes = pl.ds(pl.multiple_of(d * TOK, TOK), TOK)
             part = b.p[kv * GROUP : kv * GROUP + GROUP, :, lanes].reshape(GROUP * TOK, TOK)
@@ -342,17 +377,23 @@
             )
             return carry
 
-        lax.fori_loop(0, WIN + 1, one, 0)
+        lax.fori_loop(low, high, one, 0)
+
+    def grads_far(kv):
+        grads(kv, 3, 5)
+        send(b.dv.at[kv, 3], b.r.at[kv, 1], "r", 2 * kv + 1, sibling)
+
+    def grads_near(kv):
+        grads(kv, 1, 3)
         send(b.dv.at[kv, 1], b.r.at[kv, 0], "r", 2 * kv, sibling)
-        send(b.dv.at[kv, 3], b.r.at[kv, 1], "r", 2 * kv + 1, sibling)
 
     def leave_far(kv):
-        arrived(b.r.at[kv, 0], "r", 2 * kv)
         arrived(b.r.at[kv, 1], "r", 2 * kv + 1)
         b.fo[kv] = (b.dv[kv, 4] + b.r[kv, 2 - c]).astype(BF)
         send(b.fo.at[kv], b.fi.at[kv], "f", kv, preceding)
 
     def leave_near(kv):
+        arrived(b.r.at[kv, 0], "r", 2 * kv)
         arrived(b.fi.at[kv], "f", kv)
         b.go[kv] = (b.dv[kv, 2] + b.r[kv, 1 - c] + b.fi[kv].astype(F32)).astype(BF)
         send(b.go.at[kv], b.gi.at[kv], "g", kv, preceding)
@@ -391,29 +432,39 @@
         for k in range(4):
             arrived(vg_at(kv, y, c), "vd", 4 * kv + k)
 
-    grads(0)
-    grads(1)
+    grads_far(0)
+    grads_far(1)
     leave_far(0)
-    grads(2)
+    grads_far(2)
     leave_far(1)
-    grads(3)
+    grads_far(3)
     leave_far(2)
+    grads_near(0)
     leave_far(3)
-    for kv in range(KV):
-        leave_near(kv)
+    grads_near(1)
+    grads_near(2)
+    leave_near(0)
+    grads_near(3)
+    leave_near(1)
+    grads(0, 0, 1)
+    grads(1, 0, 1)
+    leave_near(2)
+    grads(2, 0, 1)
+    grads(3, 0, 1)
+    leave_near(3)
+    kept.wait()
+    for k in (0, 2, 3, 4, 5):
+        arrived(b.ex.at[0], "e", k)
+    for k in range(12, 16):
+        arrived(b.er.at[0, 0], "e", k)
+
     settle(0)
     settle(1)
+    settle(2)
     relay(0)
-    settle(2)
+    settle(3)
     relay(1)
     collect(0)
-
-    kept.wait()
-    arrived(b.ex.at[0], "e", 0)
-    for d in range(2, 8):
-        arrived(b.ex.at[0], "e", d)
-
-    settle(3)
     relay(2)
     collect(1)
     complete(0)
@@ -477,8 +528,8 @@
             total = total + b.rz[h, zs]
         out[:, h * 256 : (h + 1) * 256] = total
 
+    relay(3)
     product(0)
-    relay(3)
     collect(2)
     across(0)
     collect(3)

time: 122 us -> 124 us (1.016)
    pallas_call x1, Pallas kernels: 120 us -> 121 us  [weight_gradient(): pl.pallas_call(kernel, out_shape=jax.ShapeDtypeStruct((16, 512), F32), in...]
where the time goes in v2:
time: 124 us; the launch traced here: 123 us
  Pallas kernels  121 us (98%)
  other arithmetic  1.42 us (1%)
    pallas_call x1, Pallas kernels, weight_gradient(): pl.pallas_call(kernel, out_shape=jax.ShapeDtypeStruct((16, 512), F32), in...  121 us

profile of v2, /device:TPU:1, one launch (start us, length us, event | category | flops | bytes accessed | tf_op | source)
XLA Modules:
  0.0 123.5 jit_solution(10468299837705018505)
XLA Ops:
  0.6 0.0 copy-start
  0.6 0.0 copy-start.1
  0.7 0.0 copy-start.2
  0.7 0.0 copy-start.3
  0.7 121.3 %shard_map.129 = f32[16,512]{1,0:T(8,128)} custom-call(s32[1,5]{1,0:T(1,128)} %bitcast.9, s32[1,256]{1,0:T(1,128)} %doc.1, bf16[256,4096]{1,0:T(8,128)(2,1)} %bitcast.5, bf16[256,2048]{1,0:T(8,128)(2,1)} %bitcast.6, bf16[256,512]{1,0:T(8,128)(2,1)} %bitcast.8, bf16[256,2048]{1,0:T(8,128)(2,1)} %bitcast.7, bf16[16,512]{1,0:T(8,128)(2,1)} %yw_h.1), custom_call_target="tpu_custom_call" | custom-call | tf_op jit(solution)/shard_map/pallas_call | solution.py:561
  122.0 0.0 copy-done
  122.0 0.0 copy-done.1
  122.0 0.0 copy-done.2
  122.0 0.0 copy-done.3
  122.1 1.4 %add_convert_fusion = (bf16[16,512]{1,0:T(8,128)(2,1)}, f32[16,512]{1,0:T(8,128)}, f32[16,512]{1,0:T(8,128)}, f32[16,512]{1,0:T(8,128)}) fusion(f32[16,512]{1,0:T(8,128)S(1)} %copy-done.1, f32[16,512]{1,0:T(8,128)S(1)} %copy-done.2, bf16[16,512]{1,0:T(8,128)(2,1)S(1)} %copy-done, f32[16,512]{1,0:T(8,128)} %shard_map.129, f32[16,512]{1,0:T(8,128)S(1)} %copy-done.3), kind=kLoop, calls=%fused_computation.2 | loop fusion | flops 147456 | bytes 262144 | tf_op jit(solution)/shard_map/convert_element_type | solution.py:595
Async XLA Ops:
  0.6 121.4 %copy-start = (bf16[16,512]{1,0:T(8,128)(2,1)S(1)}, bf16[16,512]{1,0:T(8,128)(2,1)}, u32[]{:S(2)}) copy-start(bf16[16,512]{1,0:T(8,128)(2,1)} %yw_h.1) | copy-start | bytes 49156
  0.6 121.4 %copy-start.1 = (f32[16,512]{1,0:T(8,128)S(1)}, f32[16,512]{1,0:T(8,128)}, u32[]{:S(2)}) copy-start(f32[16,512]{1,0:T(8,128)} %param.18) | copy-start | bytes 98308
  0.7 121.4 %copy-start.2 = (f32[16,512]{1,0:T(8,128)S(1)}, f32[16,512]{1,0:T(8,128)}, u32[]{:S(2)}) copy-start(f32[16,512]{1,0:T(8,128)} %param.17) | copy-start | bytes 98308
  0.7 121.4 %copy-start.3 = (f32[16,512]{1,0:T(8,128)S(1)}, f32[16,512]{1,0:T(8,128)}, u32[]{:S(2)}) copy-start(f32[16,512]{1,0:T(8,128)} %param.19) | copy-start | bytes 98308

commit v3 on v2

--- a/solution.py
+++ b/solution.py
@@ -53,13 +53,14 @@
     "go": ((KV, TOK, HEAD), BF),
     "gi": ((KV, TOK, HEAD), BF),
     "vg": ((2, 8, TOK, 256), BF),
-    "er": ((2, 2, 128, 512), BF),
-    "ex": ((8, TOK, 512), BF),
-    "g": ((2, 4, 2, NX, 16, 256), F32),
-    "x1": ((2, 2, 2, 2, 16, 256), F32),
-    "tx": ((2, 2, 4, 2, 16, 256), F32),
-    "x2": ((2, 2, 4, 2, 16, 256), F32),
-    "t": ((2, 4, 2, 16, 256), F32),
+    "et": ((NY, NZ, 2, NX, 16, TOK), BF),
+    "er": ((2, 2, 2, NZ, 16, TOK), BF),
+    "ex": ((NY, NZ, 16, 8 * TOK), BF),
+    "g": ((2, NY, NZ, 16, 256), F32),
+    "x1": ((2, 2, 4, 16, 256), F32),
+    "tx": ((2, 2, NZ, 16, 256), F32),
+    "x2": ((2, 2, NZ, 16, 256), F32),
+    "t": ((2, NZ, 16, 256), F32),
     "rz": ((2, NZ, 16, 256), F32),
 }
 SEMAPHORES = {
@@ -68,7 +69,7 @@
     "w2": 6,
     "w3": 8,
     "wd": 10,
-    "k": 4,
+    "k": 8,
     "v": 16,
     "e": 16,
     "r": 8,
@@ -141,12 +142,12 @@
     barrier = pltpu.get_barrier_semaphore()
     partners = [sibling, following, preceding]
     for d in range(1, NZ):
+        partners.append(dev(cp_1=lax.rem(z + d, NZ)))
+    for d in range(1, NY):
+        partners.append(dev(cp_0=lax.rem(y + d, NY)))
+    for d in range(1, NX):
         for cc in (c, o):
-            partners.append(dev(cp_1=lax.rem(z + d, NZ), cp_2=cc))
-    for d in range(1, NY):
-        for cc in (c, o):
-            partners.append(dev(cp_0=lax.rem(y + d, NY), cp_2=cc))
-        partners.append(dev(fs=lax.rem(x + d, NX)))
+            partners.append(dev(fs=lax.rem(x + d, NX), cp_2=cc))
     for who in partners:
         pl.semaphore_signal(barrier, inc=1, device_id=who, device_id_type=MESH)
     pl.semaphore_wait(barrier, len(partners))
@@ -155,8 +156,6 @@
     loads["w1"].wait()
     for d in range(1, NZ):
         send(mine, mine, "w1", d, dev(cp_1=lax.rem(z + d, NZ)))
-    loads["k"].wait()
-    send(b.kw.at[0], b.kw.at[2], "k", 0, following)
 
     doc_t = jnp.transpose(jnp.broadcast_to(doc[...], (TOK, TOK)))
     row = lax.broadcasted_iota(jnp.int32, (TOK, TOK), 0) + block * TOK
@@ -172,6 +171,14 @@
     for kv in range(KV):
         b.r[kv, 2] = jnp.zeros((TOK, HEAD), F32)
 
+    def turn(e, carry):
+        lanes = pl.ds(pl.multiple_of(e * 512, 512), 512)
+        turned = jnp.transpose(b.emb[:, lanes]).reshape(4, 2, NX, 16, TOK)
+        b.et[lax.div(e, 2), pl.ds(4 * lax.rem(e, 2), 4)] = turned
+        return carry
+
+    loads["emb"].wait()
+
     for d in range(1, NZ):
         arrived(mine, "w1", d)
     first, second = b.w.at[0, y, :, c, x], b.w.at[1, y, :, c, x]
@@ -179,6 +186,8 @@
         send(first, first, "w2", d - 1, dev(cp_0=lax.rem(y + d, NY)))
         send(second, second, "w2", d + 2, dev(fs=lax.rem(x + d, NX)))
 
+    lax.fori_loop(0, 8, turn, 0)
+
     for d in range(6):
         arrived(first, "w2", d)
 
@@ -199,30 +208,50 @@
     send(half_b(y), half_b(y), "w3", 2, dev(cp_0=yup))
     send(half_b(y), half_b(y), "w3", 3, dev(cp_0=ydn))
 
-    arrived(b.kw.at[2], "k", 0)
-    send(b.kw.at[2], b.kw.at[4], "k", 1, following)
-    send(b.kw.at[2 * c], b.kw.at[1], "k", 2, sibling)
     send(half_a(x), half_a(x), "wd", 0, sibling)
     send(half_b(y), half_b(y), "wd", 1, sibling)
 
-    arrived(b.kw.at[4], "k", 1)
-    send(b.kw.at[2 + 2 * c], b.kw.at[3], "k", 3, sibling)
+    loads["k"].wait()
+
+    def keys_at(d, s):
+        return b.kw.at[d, 128 * s : 128 * s + 128]
+
+    def pass_keys(s):
+        arrived(keys_at(2, s), "k", s)
+        send(keys_at(2, s), keys_at(4, s), "k", 2 + s, following)
+        send(keys_at(2 * c, s), keys_at(1, s), "k", 4 + s, sibling)
+
+    keys_out = [copy(keys_at(0, s), keys_at(2, s), "k", s, following) for s in range(2)]
+    started.extend(keys_out)
+
+    @pl.when(z != NZ - 1)
+    def _():
+        for made in keys_out:
+            made.start()
 
     arrived(half_a(x), "w3", 0)
     send(relay_a(xdn, 0), relay_a(xdn, 0), "w3", 4, dev(fs=xup))
     arrived(half_a(x), "w3", 1)
     send(relay_a(xup, 1), relay_a(xup, 1), "w3", 5, dev(fs=xdn))
-    arrived(half_b(y), "w3", 2)
-    send(relay_b(ydn, 0), relay_b(ydn, 0), "w3", 6, dev(cp_0=yup))
     arrived(half_b(y), "w3", 3)
-    send(relay_b(yup, 1), relay_b(yup, 1), "w3", 7, dev(cp_0=ydn))
+    for s in range(2):
+        send(relay_b(yup, s), relay_b(yup, s), "w3", 6 + s, dev(cp_0=ydn))
     send(half_a(xdn), half_a(xdn), "wd", 2, sibling)
     send(half_a(xup), half_a(xup), "wd", 3, sibling)
+    send(half_b(yup), half_b(yup), "wd", 5, sibling)
+
+    @pl.when(z == NZ - 1)
+    def _():
+        for made in keys_out:
+            made.start()
+
+    arrived(half_b(y), "w3", 2)
     send(half_b(ydn), half_b(ydn), "wd", 4, sibling)
-    send(half_b(yup), half_b(yup), "wd", 5, sibling)
-
-    arrived(b.kw.at[1], "k", 2)
-    arrived(b.kw.at[3], "k", 3)
+    pass_keys(0)
+    pass_keys(1)
+    for s in range(2):
+        arrived(keys_at(4, s), "k", 2 + s)
+        send(keys_at(2 + 2 * c, s), keys_at(3, s), "k", 6 + s, sibling)
     loads["q"].wait()
 
     def head_probs(hd, carry):
@@ -241,15 +270,12 @@
             b.p[hd, rows, :] = (weight * (1.0 / total)).astype(BF)
         return carry
 
-    lax.fori_loop(0, 6, head_probs, 0)
-
     for s in range(2):
         arrived(relay_a(x, s), "w3", 4 + s)
         send(relay_a(xop, s), relay_a(xop, s), "wd", 6 + s, sibling)
     for s in range(2):
         arrived(relay_b(y, s), "w3", 6 + s)
         send(relay_b(yop, s), relay_b(yop, s), "wd", 8 + s, sibling)
-    lax.fori_loop(6, 8, head_probs, 0)
     for k in (0, 2, 3):
         arrived(half_a(x), "wd", k)
     for k in (1, 4, 5):
@@ -258,7 +284,29 @@
         arrived(relay_a(x, s), "wd", 6 + s)
         arrived(relay_b(y, s), "wd", 8 + s)
 
-    loads["emb"].wait()
+    def columns_of(blk):
+        return pl.ds(pl.multiple_of(blk * TOK, TOK), TOK)
+
+    own = x * 2 + c
+    here = b.ex.at[:, :, :, columns_of(own)]
+    kept = pltpu.make_async_copy(b.et.at[:, :, c, x], here, rcv["ld"].at[14])
+    kept.start()
+    send(b.et.at[:, :, o, x], here, "e", 0, sibling)
+    for s, xt in enumerate((xup, xdn)):
+        for k, cc in enumerate((c, o)):
+            part = b.et.at[2 * s : 2 * s + 2, :, cc, xop]
+            send(part, b.er.at[s, k], "e", 8 + 2 * s + k, dev(fs=xt))
+    for s, xt in enumerate((xup, xdn)):
+        for k, cc in enumerate((c, o)):
+            send(b.et.at[:, :, cc, xt], here, "e", 2 + 2 * s + k, dev(fs=xt, cp_2=cc))
+
+    def pass_embeds():
+        for s, (xt, xf) in enumerate(((xup, xdn), (xdn, xup))):
+            for k, cc in enumerate((c, o)):
+                arrived(b.er.at[s, k], "e", 8 + 2 * s + k)
+                there = b.ex.at[2 * s : 2 * s + 2, :, :, columns_of(xf * 2 + c)]
+                send(b.er.at[s, k], there, "e", 12 + 2 * s + k, dev(fs=xt, cp_2=cc))
+
     for h in range(2):
         made = jnp.dot(b.emb[...], b.w[h].reshape(4096, 256), preferred_element_type=F32)
         for k in range(2):
@@ -266,84 +314,47 @@
             b.vw[kv, 0] = made[:, k * HEAD : (k + 1) * HEAD].astype(BF)
             send(b.vw.at[kv, 0], b.vw.at[kv, 2], "v", kv, following)
 
-    def emb_at(yy, cc):
-        return b.emb.at[:, pl.ds(pl.multiple_of((yy * 2 + cc) * 512, 512), 512)]
-
-    def emb_part(yy, cc, s):
-        return b.emb.at[
-            128 * s : 128 * s + 128, pl.ds(pl.multiple_of((yy * 2 + cc) * 512, 512), 512)
-        ]
-
-    own = y * 2 + c
-    kept = pltpu.make_async_copy(emb_at(y, c), b.ex.at[own], rcv["ld"].at[14])
-    kept.start()
-    send(emb_at(y, o), b.ex.at[own], "e", 0, sibling)
-    for s, yt in enumerate((yup, ydn)):
-        for k, cc in enumerate((c, o)):
-            send(emb_part(yop, cc, s), b.er.at[s, k], "e", 8 + 2 * s + k, dev(cp_0=yt))
-    for s, yt in enumerate((yup, ydn)):
-        for k, cc in enumerate((c, o)):
-            send(emb_at(yt, cc), b.ex.at[own], "e", 2 + 2 * s + k, dev(cp_0=yt, cp_2=cc))
-
-    def pass_embeds():
-        for s, (yt, yf) in enumerate(((yup, ydn), (ydn, yup))):
-            for k, cc in enumerate((c, o)):
-                arrived(b.er.at[s, k], "e", 8 + 2 * s + k)
-                send(
-                    b.er.at[s, k],
-                    b.ex.at[yf * 2 + c, 128 * s : 128 * s + 128],
-                    "e",
-                    12 + 2 * s + k,
-                    dev(cp_0=yt, cp_2=cc),
-                )
-
-    lax.fori_loop(8, 12, head_probs, 0)
-    for kv in range(KV):
+    def pass_near(kv):
         arrived(b.vw.at[kv, 2], "v", kv)
         send(b.vw.at[kv, 2], b.vw.at[kv, 4], "v", 4 + kv, following)
         send(b.vw.at[kv, 2 * c], b.vw.at[kv, 1], "v", 8 + kv, sibling)
-    lax.fori_loop(12, 16, head_probs, 0)
-    near, far = 3 * TOK, 2 * TOK
-
-    def attend_near(kv):
+
+    def pass_far(kv):
+        arrived(b.vw.at[kv, 4], "v", 4 + kv)
+        send(b.vw.at[kv, 2 + 2 * c], b.vw.at[kv, 3], "v", 12 + kv, sibling)
+
+    def attend(kv):
         arrived(b.vw.at[kv, 1], "v", 8 + kv)
+        arrived(b.vw.at[kv, 3], "v", 12 + kv)
 
         def one(k, carry):
             hd = kv * GROUP + k
-            values = b.vw[kv, 0:3].reshape(near, HEAD)
-            b.att[hd] = jnp.dot(b.p[hd, :, 0:near], values, preferred_element_type=F32)
+            values = b.vw[kv].reshape(SPAN, HEAD)
+            b.att[hd] = jnp.dot(b.p[hd], values, preferred_element_type=F32)
             return carry
 
         lax.fori_loop(0, GROUP, one, 0)
 
-    def attend_far(kv):
-        arrived(b.vw.at[kv, 3], "v", 12 + kv)
-
-        def one(k, carry):
-            hd = kv * GROUP + k
-            values = b.vw[kv, 3:5].reshape(far, HEAD)
-            b.att[hd] += jnp.dot(b.p[hd, :, near:SPAN], values, preferred_element_type=F32)
-            return carry
-
-        lax.fori_loop(0, GROUP, one, 0)
-
-    def pass_values(kv):
-        arrived(b.vw.at[kv, 4], "v", 4 + kv)
-        send(b.vw.at[kv, 2 + 2 * c], b.vw.at[kv, 3], "v", 12 + kv, sibling)
-
-    attend_near(0)
-    attend_near(1)
-    pass_values(0)
-    attend_near(2)
-    attend_near(3)
-    pass_values(1)
-    attend_far(0)
-    pass_values(2)
-    attend_far(1)
+    for s in range(2):
+        arrived(keys_at(1, s), "k", 4 + s)
+        arrived(keys_at(3, s), "k", 6 + s)
+    lax.fori_loop(0, 7, head_probs, 0)
+    pass_near(0)
+    pass_near(1)
+    lax.fori_loop(7, 9, head_probs, 0)
+    pass_near(2)
+    lax.fori_loop(9, 11, head_probs, 0)
+    pass_near(3)
     pass_embeds()
-    pass_values(3)
-    attend_far(2)
-    attend_far(3)
+    lax.fori_loop(11, 16, head_probs, 0)
+    pass_far(0)
+    pass_far(1)
+    attend(0)
+    pass_far(2)
+    attend(1)
+    pass_far(3)
+    attend(2)
+    attend(3)
 
     loads["cot"].wait()
     token_total = TOK * NY * NZ * 2 * NX
@@ -398,39 +409,39 @@
         b.go[kv] = (b.dv[kv, 2] + b.r[kv, 1 - c] + b.fi[kv].astype(F32)).astype(BF)
         send(b.go.at[kv], b.gi.at[kv], "g", kv, preceding)
 
-    def vg_at(kv, yy, cc, rows=slice(None)):
+    def vg_at(kv, xx, cc, rows=slice(None)):
         lanes = slice((kv % 2) * HEAD, (kv % 2) * HEAD + HEAD)
-        return b.vg.at[kv // 2, yy * 2 + cc, rows, lanes]
+        return b.vg.at[kv // 2, xx * 2 + cc, rows, lanes]
 
     upper, lower = slice(0, 128), slice(128, 256)
 
     def settle(kv):
         arrived(b.gi.at[kv], "g", kv)
         total = b.dv[kv, 0] + b.r[kv, 2 * c] + b.gi[kv].astype(F32)
-        b.vg[kv // 2, own, :, (kv % 2) * HEAD : (kv % 2) * HEAD + HEAD] = total.astype(BF)
-        here = vg_at(kv, y, c)
-        send(here, here, "vg", 4 * kv, dev(cp_0=yup))
-        send(here, here, "vg", 4 * kv + 1, dev(cp_0=ydn))
-        send(here, here, "vd", 4 * kv, sibling)
+        b.vg[kv // 2, x * 2 + c, :, (kv % 2) * HEAD : (kv % 2) * HEAD + HEAD] = total.astype(BF)
+        mine = vg_at(kv, x, c)
+        send(mine, mine, "vg", 4 * kv, dev(fs=xup))
+        send(mine, mine, "vg", 4 * kv + 1, dev(fs=xdn))
+        send(mine, mine, "vd", 4 * kv, sibling)
 
     def relay(kv):
-        arrived(vg_at(kv, y, c), "vg", 4 * kv)
-        part = vg_at(kv, ydn, c, upper)
-        send(part, part, "vg", 4 * kv + 2, dev(cp_0=yup))
-        send(vg_at(kv, ydn, c), vg_at(kv, ydn, c), "vd", 4 * kv + 1, sibling)
-        arrived(vg_at(kv, y, c), "vg", 4 * kv + 1)
-        part = vg_at(kv, yup, c, lower)
-        send(part, part, "vg", 4 * kv + 3, dev(cp_0=ydn))
-        send(vg_at(kv, yup, c), vg_at(kv, yup, c), "vd", 4 * kv + 2, sibling)
+        arrived(vg_at(kv, x, c), "vg", 4 * kv)
+        part = vg_at(kv, xdn, c, upper)
+        send(part, part, "vg", 4 * kv + 2, dev(fs=xup))
+        send(vg_at(kv, xdn, c), vg_at(kv, xdn, c), "vd", 4 * kv + 1, sibling)
+        arrived(vg_at(kv, x, c), "vg", 4 * kv + 1)
+        part = vg_at(kv, xup, c, lower)
+        send(part, part, "vg", 4 * kv + 3, dev(fs=xdn))
+        send(vg_at(kv, xup, c), vg_at(kv, xup, c), "vd", 4 * kv + 2, sibling)
 
     def collect(kv):
-        arrived(vg_at(kv, y, c, upper), "vg", 4 * kv + 2)
-        arrived(vg_at(kv, y, c, lower), "vg", 4 * kv + 3)
-        send(vg_at(kv, yop, c), vg_at(kv, yop, c), "vd", 4 * kv + 3, sibling)
+        arrived(vg_at(kv, x, c, upper), "vg", 4 * kv + 2)
+        arrived(vg_at(kv, x, c, lower), "vg", 4 * kv + 3)
+        send(vg_at(kv, xop, c), vg_at(kv, xop, c), "vd", 4 * kv + 3, sibling)
 
     def complete(kv):
         for k in range(4):
-            arrived(vg_at(kv, y, c), "vd", 4 * kv + k)
+            arrived(vg_at(kv, x, c), "vd", 4 * kv + k)
 
     grads_far(0)
     grads_far(1)
@@ -454,7 +465,7 @@
     leave_near(3)
     kept.wait()
     for k in (0, 2, 3, 4, 5):
-        arrived(b.ex.at[0], "e", k)
+        arrived(here, "e", k)
     for k in range(12, 16):
         arrived(b.er.at[0, 0], "e", k)
 
@@ -471,61 +482,38 @@
     complete(1)
 
     def product(h):
-        grad = lax.dot_general(
-            b.ex[...].reshape(8 * TOK, 512),
+        grad = jnp.dot(
+            b.ex[...].reshape(512, 8 * TOK),
             b.vg[h].reshape(8 * TOK, 256),
-            (((0,), (0,)), ((), ())),
             preferred_element_type=F32,
         )
-        b.g[h] = grad.reshape(4, 2, NX, 16, 256)
-        send(b.g.at[h, 0:2, :, xop], b.x1.at[h, 0], "x", 4 * h, dev(fs=xup))
-        send(b.g.at[h, 2:4, :, xop], b.x1.at[h, 1], "x", 4 * h + 1, dev(fs=xdn))
+        b.g[h] = grad.reshape(NY, NZ, 16, 256)
+        send(b.g.at[h, yop, 0:4], b.x1.at[h, 0], "x", 4 * h, dev(cp_0=yup))
+        send(b.g.at[h, yop, 4:8], b.x1.at[h, 1], "x", 4 * h + 1, dev(cp_0=ydn))
 
     def across(h):
         arrived(b.x1.at[h, 0], "x", 4 * h)
-        b.tx[h, 0, 0:2] = b.g[h, 0:2, :, xup] + b.x1[h, 0]
-        b.tx[h, 0, 2:4] = b.g[h, 2:4, :, xup]
-        send(b.tx.at[h, 0], b.x2.at[h, 0], "x", 4 * h + 2, dev(fs=xup))
+        b.tx[h, 0, 0:4] = b.g[h, yup, 0:4] + b.x1[h, 0]
+        b.tx[h, 0, 4:8] = b.g[h, yup, 4:8]
+        send(b.tx.at[h, 0], b.x2.at[h, 0], "x", 4 * h + 2, dev(cp_0=yup))
         arrived(b.x1.at[h, 1], "x", 4 * h + 1)
-        b.tx[h, 1, 0:2] = b.g[h, 0:2, :, xdn]
-        b.tx[h, 1, 2:4] = b.g[h, 2:4, :, xdn] + b.x1[h, 1]
-        send(b.tx.at[h, 1], b.x2.at[h, 1], "x", 4 * h + 3, dev(fs=xdn))
+        b.tx[h, 1, 0:4] = b.g[h, ydn, 0:4]
+        b.tx[h, 1, 4:8] = b.g[h, ydn, 4:8] + b.x1[h, 1]
+        send(b.tx.at[h, 1], b.x2.at[h, 1], "x", 4 * h + 3, dev(cp_0=ydn))
 
     def along(h):
         arrived(b.x2.at[h, 0], "x", 4 * h + 2)
         arrived(b.x2.at[h, 1], "x", 4 * h + 3)
-        b.t[h] = b.g[h, :, :, x] + b.x2[h, 0] + b.x2[h, 1]
-        for k in range(4):
-            for cc in range(2):
-                zt = 4 * c + k
-                stays = jnp.logical_and(zt == z, c == cc)
-
-                @pl.when(stays)
-                def _():
-                    b.rz[h, z] = b.t[h, k, cc]
-
-                @pl.when(jnp.logical_not(stays))
-                def _():
-                    pltpu.make_async_remote_copy(
-                        src_ref=b.t.at[h, k, cc],
-                        dst_ref=b.rz.at[h, z],
-                        send_sem=snd["z"].at[8 * h + 2 * k + cc],
-                        recv_sem=rcv["z"].at[8 * h + z],
-                        device_id=dev(cp_1=zt, cp_2=cc),
-                        device_id_type=MESH,
-                    ).start()
+        b.t[h] = b.g[h, y] + b.x2[h, 0] + b.x2[h, 1]
+        for d in (4, 3, 5, 2, 6, 1, 7):
+            zt = lax.rem(z + d, NZ)
+            send(b.t.at[h, zt], b.rz.at[h, z], "z", 8 * h + d, dev(cp_1=zt))
 
     def finish(h):
-        for zs in range(NZ):
-            stays = jnp.logical_and(zs == z, lax.div(z, 4) == c)
-
-            @pl.when(jnp.logical_not(stays))
-            def _():
-                arrived(b.rz.at[h, 0], "z", 8 * h + zs)
-
-        total = b.rz[h, 0]
-        for zs in range(1, NZ):
-            total = total + b.rz[h, zs]
+        total = b.t[h, z]
+        for d in (1, 7, 2, 6, 3, 5, 4):
+            arrived(b.rz.at[h, 0], "z", 8 * h + d)
+            total = total + b.rz[h, lax.rem(z + NZ - d, NZ)]
         out[:, h * 256 : (h + 1) * 256] = total
 
     relay(3)
@@ -544,14 +532,6 @@
 
     for made in started:
         made.wait_send()
-    for h in range(2):
-        for k in range(4):
-            for cc in range(2):
-                stays = jnp.logical_and(4 * c + k == z, c == cc)
-
-                @pl.when(jnp.logical_not(stays))
-                def _():
-                    copy(b.t.at[h, k, cc], b.rz.at[h, 0], "z", 8 * h + 2 * k + cc, sibling).wait_send()
 
 
 def weight_gradient(need_ids, doc_start, embeds, queries, key_heads, cotangent, y_weight):

time: 124 us -> 110 us (0.89)
  Pallas kernels: 121 us -> 107 us
    pallas_call x1, Pallas kernels: 121 us -> 107 us  [weight_gradient(): pl.pallas_call(kernel, out_shape=jax.ShapeDtypeStruct((16, 512), F32), in...]
where the time goes in v3:
time: 110 us; the launch traced here: 109 us
  Pallas kernels  107 us (97%)
  other arithmetic  1.42 us (1%)
    pallas_call x1, Pallas kernels, weight_gradient(): pl.pallas_call(kernel, out_shape=jax.ShapeDtypeStruct((16, 512), F32), in...  107 us

profile of v3, /device:TPU:1, one launch (start us, length us, event | category | flops | bytes accessed | tf_op | source)
XLA Modules:
  0.0 108.8 jit_solution(14155591181935245854)
XLA Ops:
  0.6 0.0 copy-start
  0.6 0.0 copy-start.1
  0.7 0.0 copy-start.2
  0.7 0.0 copy-start.3
  0.7 106.6 %shard_map.129 = f32[16,512]{1,0:T(8,128)} custom-call(s32[1,5]{1,0:T(1,128)} %bitcast.9, s32[1,256]{1,0:T(1,128)} %doc.1, bf16[256,4096]{1,0:T(8,128)(2,1)} %bitcast.5, bf16[256,2048]{1,0:T(8,128)(2,1)} %bitcast.6, bf16[256,512]{1,0:T(8,128)(2,1)} %bitcast.8, bf16[256,2048]{1,0:T(8,128)(2,1)} %bitcast.7, bf16[16,512]{1,0:T(8,128)(2,1)} %yw_h.1), custom_call_target="tpu_custom_call" | custom-call | tf_op jit(solution)/shard_map/pallas_call | solution.py:541
  107.3 0.0 copy-done
  107.3 0.0 copy-done.1
  107.3 0.0 copy-done.2
  107.3 0.0 copy-done.3
  107.3 1.4 %add_convert_fusion = (bf16[16,512]{1,0:T(8,128)(2,1)}, f32[16,512]{1,0:T(8,128)}, f32[16,512]{1,0:T(8,128)}, f32[16,512]{1,0:T(8,128)}) fusion(f32[16,512]{1,0:T(8,128)S(1)} %copy-done.1, f32[16,512]{1,0:T(8,128)S(1)} %copy-done.2, bf16[16,512]{1,0:T(8,128)(2,1)S(1)} %copy-done, f32[16,512]{1,0:T(8,128)} %shard_map.129, f32[16,512]{1,0:T(8,128)S(1)} %copy-done.3), kind=kLoop, calls=%fused_computation.2 | loop fusion | flops 147456 | bytes 262144 | tf_op jit(solution)/shard_map/convert_element_type | solution.py:575
Async XLA Ops:
  0.6 106.7 %copy-start = (bf16[16,512]{1,0:T(8,128)(2,1)S(1)}, bf16[16,512]{1,0:T(8,128)(2,1)}, u32[]{:S(2)}) copy-start(bf16[16,512]{1,0:T(8,128)(2,1)} %yw_h.1) | copy-start | bytes 49156
  0.6 106.7 %copy-start.1 = (f32[16,512]{1,0:T(8,128)S(1)}, f32[16,512]{1,0:T(8,128)}, u32[]{:S(2)}) copy-start(f32[16,512]{1,0:T(8,128)} %param.18) | copy-start | bytes 98308
  0.7 106.7 %copy-start.2 = (f32[16,512]{1,0:T(8,128)S(1)}, f32[16,512]{1,0:T(8,128)}, u32[]{:S(2)}) copy-start(f32[16,512]{1,0:T(8,128)} %param.17) | copy-start | bytes 98308
  0.7 106.7 %copy-start.3 = (f32[16,512]{1,0:T(8,128)S(1)}, f32[16,512]{1,0:T(8,128)}, u32[]{:S(2)}) copy-start(f32[16,512]{1,0:T(8,128)} %param.19) | copy-start | bytes 98308

commit v4 on v3

--- a/solution.py
+++ b/solution.py
@@ -45,6 +45,8 @@
     "s": ((TOK, SPAN), F32),
     "bias": ((TOK, SPAN), F32),
     "att": ((16, TOK, HEAD), F32),
+    "sq": ((TOK, HEAD), F32),
+    "cr": ((TOK, HEAD), F32),
     "og": ((16, TOK, HEAD), BF),
     "dv": ((KV, 5, TOK, HEAD), F32),
     "r": ((KV, 3, TOK, HEAD), F32),
@@ -57,11 +59,13 @@
     "er": ((2, 2, 2, NZ, 16, TOK), BF),
     "ex": ((NY, NZ, 16, 8 * TOK), BF),
     "g": ((2, NY, NZ, 16, 256), F32),
-    "x1": ((2, 2, 4, 16, 256), F32),
-    "tx": ((2, 2, NZ, 16, 256), F32),
-    "x2": ((2, 2, NZ, 16, 256), F32),
+    "g1": ((2, NZ, 16, 256), BF),
+    "x1": ((2, 2, 4, 16, 256), BF),
+    "tx": ((2, 2, NZ, 16, 256), BF),
+    "x2": ((2, 2, NZ, 16, 256), BF),
     "t": ((2, NZ, 16, 256), F32),
-    "rz": ((2, NZ, 16, 256), F32),
+    "tz": ((2, NZ, 16, 256), BF),
+    "rz": ((2, NZ, 16, 256), BF),
 }
 SEMAPHORES = {
     "ld": 16,
@@ -170,6 +174,8 @@
         b.bias[:, d * TOK : (d + 1) * TOK] = jnp.where(seen, 0.0, MASKED)
     for kv in range(KV):
         b.r[kv, 2] = jnp.zeros((TOK, HEAD), F32)
+    b.sq[...] = jnp.zeros((TOK, HEAD), F32)
+    b.cr[...] = jnp.zeros((TOK, HEAD), F32)
 
     def turn(e, carry):
         lanes = pl.ds(pl.multiple_of(e * 512, 512), 512)
@@ -233,26 +239,32 @@
     send(relay_a(xdn, 0), relay_a(xdn, 0), "w3", 4, dev(fs=xup))
     arrived(half_a(x), "w3", 1)
     send(relay_a(xup, 1), relay_a(xup, 1), "w3", 5, dev(fs=xdn))
+    arrived(half_b(y), "w3", 2)
+    send(relay_b(ydn, 0), relay_b(ydn, 0), "w3", 6, dev(cp_0=yup))
     arrived(half_b(y), "w3", 3)
-    for s in range(2):
-        send(relay_b(yup, s), relay_b(yup, s), "w3", 6 + s, dev(cp_0=ydn))
-    send(half_a(xdn), half_a(xdn), "wd", 2, sibling)
-    send(half_a(xup), half_a(xup), "wd", 3, sibling)
-    send(half_b(yup), half_b(yup), "wd", 5, sibling)
+    send(relay_b(yup, 1), relay_b(yup, 1), "w3", 7, dev(cp_0=ydn))
 
     @pl.when(z == NZ - 1)
     def _():
         for made in keys_out:
             made.start()
 
-    arrived(half_b(y), "w3", 2)
+    send(half_a(xdn), half_a(xdn), "wd", 2, sibling)
+    send(half_a(xup), half_a(xup), "wd", 3, sibling)
     send(half_b(ydn), half_b(ydn), "wd", 4, sibling)
+    send(half_b(yup), half_b(yup), "wd", 5, sibling)
     pass_keys(0)
     pass_keys(1)
+    loads["q"].wait()
+    for s in range(2):
+        arrived(relay_a(x, s), "w3", 4 + s)
+        send(relay_a(xop, s), relay_a(xop, s), "wd", 6 + s, sibling)
+    for s in range(2):
+        arrived(relay_b(y, s), "w3", 6 + s)
+        send(relay_b(yop, s), relay_b(yop, s), "wd", 8 + s, sibling)
     for s in range(2):
         arrived(keys_at(4, s), "k", 2 + s)
         send(keys_at(2 + 2 * c, s), keys_at(3, s), "k", 6 + s, sibling)
-    loads["q"].wait()
 
     def head_probs(hd, carry):
         lanes = pl.ds(pl.multiple_of(hd * HEAD, HEAD), HEAD)
@@ -270,12 +282,6 @@
             b.p[hd, rows, :] = (weight * (1.0 / total)).astype(BF)
         return carry
 
-    for s in range(2):
-        arrived(relay_a(x, s), "w3", 4 + s)
-        send(relay_a(xop, s), relay_a(xop, s), "wd", 6 + s, sibling)
-    for s in range(2):
-        arrived(relay_b(y, s), "w3", 6 + s)
-        send(relay_b(yop, s), relay_b(yop, s), "wd", 8 + s, sibling)
     for k in (0, 2, 3):
         arrived(half_a(x), "wd", k)
     for k in (1, 4, 5):
@@ -330,7 +336,11 @@
         def one(k, carry):
             hd = kv * GROUP + k
             values = b.vw[kv].reshape(SPAN, HEAD)
-            b.att[hd] = jnp.dot(b.p[hd], values, preferred_element_type=F32)
+            made = jnp.dot(b.p[hd], values, preferred_element_type=F32)
+            b.att[hd] = made
+            lanes = pl.ds(pl.multiple_of(hd * HEAD, HEAD), HEAD)
+            b.sq[...] += made * made
+            b.cr[...] += made * b.cot[:, lanes].astype(F32)
             return carry
 
         lax.fori_loop(0, GROUP, one, 0)
@@ -338,16 +348,18 @@
     for s in range(2):
         arrived(keys_at(1, s), "k", 4 + s)
         arrived(keys_at(3, s), "k", 6 + s)
-    lax.fori_loop(0, 7, head_probs, 0)
+    loads["cot"].wait()
+    lax.fori_loop(0, 8, head_probs, 0)
     pass_near(0)
     pass_near(1)
-    lax.fori_loop(7, 9, head_probs, 0)
+    lax.fori_loop(8, 11, head_probs, 0)
     pass_near(2)
-    lax.fori_loop(9, 11, head_probs, 0)
+    lax.fori_loop(11, 13, head_probs, 0)
     pass_near(3)
     pass_embeds()
-    lax.fori_loop(11, 16, head_probs, 0)
+    lax.fori_loop(13, 15, head_probs, 0)
     pass_far(0)
+    lax.fori_loop(15, 16, head_probs, 0)
     pass_far(1)
     attend(0)
     pass_far(2)
@@ -356,20 +368,13 @@
     attend(2)
     attend(3)
 
-    loads["cot"].wait()
     token_total = TOK * NY * NZ * 2 * NX
 
     def norm_rows(n, carry):
         rows = pl.ds(pl.multiple_of(n * 32, 32), 32)
-        squares = jnp.zeros((32, HEAD), F32)
-        crossed = jnp.zeros((32, HEAD), F32)
-        for hd in range(16):
-            a = b.att[hd, rows, :]
-            squares += a * a
-            crossed += a * b.cot[rows, hd * HEAD : (hd + 1) * HEAD].astype(F32)
-        mean = jnp.sum(squares, axis=-1, keepdims=True) / 2048.0 + NORM_EPS
+        mean = jnp.sum(b.sq[rows, :], axis=-1, keepdims=True) / 2048.0 + NORM_EPS
         inv = 1.0 / jnp.sqrt(mean)
-        inner = jnp.sum(crossed, axis=-1, keepdims=True) / (2048.0 * token_total) * inv
+        inner = jnp.sum(b.cr[rows, :], axis=-1, keepdims=True) / (2048.0 * token_total) * inv
         factor = inner * inv
         for hd in range(16):
             up = b.cot[rows, hd * HEAD : (hd + 1) * HEAD].astype(F32) / token_total
@@ -488,44 +493,46 @@
             preferred_element_type=F32,
         )
         b.g[h] = grad.reshape(NY, NZ, 16, 256)
-        send(b.g.at[h, yop, 0:4], b.x1.at[h, 0], "x", 4 * h, dev(cp_0=yup))
-        send(b.g.at[h, yop, 4:8], b.x1.at[h, 1], "x", 4 * h + 1, dev(cp_0=ydn))
+        b.g1[h] = b.g[h, yop].astype(BF)
+        send(b.g1.at[h, 0:4], b.x1.at[h, 0], "x", 4 * h, dev(cp_0=yup))
+        send(b.g1.at[h, 4:8], b.x1.at[h, 1], "x", 4 * h + 1, dev(cp_0=ydn))
 
     def across(h):
         arrived(b.x1.at[h, 0], "x", 4 * h)
-        b.tx[h, 0, 0:4] = b.g[h, yup, 0:4] + b.x1[h, 0]
-        b.tx[h, 0, 4:8] = b.g[h, yup, 4:8]
+        b.tx[h, 0, 0:4] = (b.g[h, yup, 0:4] + b.x1[h, 0].astype(F32)).astype(BF)
+        b.tx[h, 0, 4:8] = b.g[h, yup, 4:8].astype(BF)
         send(b.tx.at[h, 0], b.x2.at[h, 0], "x", 4 * h + 2, dev(cp_0=yup))
         arrived(b.x1.at[h, 1], "x", 4 * h + 1)
-        b.tx[h, 1, 0:4] = b.g[h, ydn, 0:4]
-        b.tx[h, 1, 4:8] = b.g[h, ydn, 4:8] + b.x1[h, 1]
+        b.tx[h, 1, 0:4] = b.g[h, ydn, 0:4].astype(BF)
+        b.tx[h, 1, 4:8] = (b.g[h, ydn, 4:8] + b.x1[h, 1].astype(F32)).astype(BF)
         send(b.tx.at[h, 1], b.x2.at[h, 1], "x", 4 * h + 3, dev(cp_0=ydn))
 
     def along(h):
         arrived(b.x2.at[h, 0], "x", 4 * h + 2)
         arrived(b.x2.at[h, 1], "x", 4 * h + 3)
-        b.t[h] = b.g[h, y] + b.x2[h, 0] + b.x2[h, 1]
+        b.t[h] = b.g[h, y] + b.x2[h, 0].astype(F32) + b.x2[h, 1].astype(F32)
+        b.tz[h] = b.t[h].astype(BF)
         for d in (4, 3, 5, 2, 6, 1, 7):
             zt = lax.rem(z + d, NZ)
-            send(b.t.at[h, zt], b.rz.at[h, z], "z", 8 * h + d, dev(cp_1=zt))
+            send(b.tz.at[h, zt], b.rz.at[h, z], "z", 8 * h + d, dev(cp_1=zt))
 
     def finish(h):
         total = b.t[h, z]
         for d in (1, 7, 2, 6, 3, 5, 4):
             arrived(b.rz.at[h, 0], "z", 8 * h + d)
-            total = total + b.rz[h, lax.rem(z + NZ - d, NZ)]
+            total = total + b.rz[h, lax.rem(z + NZ - d, NZ)].astype(F32)
         out[:, h * 256 : (h + 1) * 256] = total
 
     relay(3)
     product(0)
     collect(2)
-    across(0)
     collect(3)
     complete(2)
     complete(3)
     product(1)
+    across(0)
+    across(1)
     along(0)
-    across(1)
     along(1)
     finish(0)
     finish(1)

time: 110 us -> 117 us (1.064)
  Pallas kernels: 107 us -> 114 us
    pallas_call x1, Pallas kernels: 107 us -> 114 us  [weight_gradient(): pl.pallas_call(kernel, out_shape=jax.ShapeDtypeStruct((16, 512), F32), in...]
where the time goes in v4:
time: 117 us; the launch traced here: 116 us
  Pallas kernels  114 us (97%)
  other arithmetic  1.42 us (1%)
    pallas_call x1, Pallas kernels, weight_gradient(): pl.pallas_call(kernel, out_shape=jax.ShapeDtypeStruct((16, 512), F32), in...  114 us

profile of v4, /device:TPU:1, one launch (start us, length us, event | category | flops | bytes accessed | tf_op | source)
XLA Modules:
  0.0 115.7 jit_solution(3243008779047514910)
XLA Ops:
  0.6 0.0 copy-start
  0.6 0.0 copy-start.1
  0.7 0.0 copy-start.2
  0.7 0.0 copy-start.3
  0.7 113.5 %shard_map.129 = f32[16,512]{1,0:T(8,128)} custom-call(s32[1,5]{1,0:T(1,128)} %bitcast.9, s32[1,256]{1,0:T(1,128)} %doc.1, bf16[256,4096]{1,0:T(8,128)(2,1)} %bitcast.5, bf16[256,2048]{1,0:T(8,128)(2,1)} %bitcast.6, bf16[256,512]{1,0:T(8,128)(2,1)} %bitcast.8, bf16[256,2048]{1,0:T(8,128)(2,1)} %bitcast.7, bf16[16,512]{1,0:T(8,128)(2,1)} %yw_h.1), custom_call_target="tpu_custom_call" | custom-call | tf_op jit(solution)/shard_map/pallas_call | solution.py:548
  114.2 0.0 copy-done
  114.2 0.0 copy-done.1
  114.2 0.0 copy-done.2
  114.2 0.0 copy-done.3
  114.2 1.4 %add_convert_fusion = (bf16[16,512]{1,0:T(8,128)(2,1)}, f32[16,512]{1,0:T(8,128)}, f32[16,512]{1,0:T(8,128)}, f32[16,512]{1,0:T(8,128)}) fusion(f32[16,512]{1,0:T(8,128)S(1)} %copy-done.1, f32[16,512]{1,0:T(8,128)S(1)} %copy-done.2, bf16[16,512]{1,0:T(8,128)(2,1)S(1)} %copy-done, f32[16,512]{1,0:T(8,128)} %shard_map.129, f32[16,512]{1,0:T(8,128)S(1)} %copy-done.3), kind=kLoop, calls=%fused_computation.2 | loop fusion | flops 147456 | bytes 262144 | tf_op jit(solution)/shard_map/convert_element_type | solution.py:582
Async XLA Ops:
  0.6 113.6 %copy-start = (bf16[16,512]{1,0:T(8,128)(2,1)S(1)}, bf16[16,512]{1,0:T(8,128)(2,1)}, u32[]{:S(2)}) copy-start(bf16[16,512]{1,0:T(8,128)(2,1)} %yw_h.1) | copy-start | bytes 49156
  0.6 113.6 %copy-start.1 = (f32[16,512]{1,0:T(8,128)S(1)}, f32[16,512]{1,0:T(8,128)}, u32[]{:S(2)}) copy-start(f32[16,512]{1,0:T(8,128)} %param.18) | copy-start | bytes 98308
  0.7 113.6 %copy-start.2 = (f32[16,512]{1,0:T(8,128)S(1)}, f32[16,512]{1,0:T(8,128)}, u32[]{:S(2)}) copy-start(f32[16,512]{1,0:T(8,128)} %param.17) | copy-start | bytes 98308
  0.7 113.6 %copy-start.3 = (f32[16,512]{1,0:T(8,128)S(1)}, f32[16,512]{1,0:T(8,128)}, u32[]{:S(2)}) copy-start(f32[16,512]{1,0:T(8,128)} %param.19) | copy-start | bytes 98308

commit v5 on v4

--- a/solution.py
+++ b/solution.py
@@ -65,33 +65,34 @@
     "x2": ((2, 2, NZ, 16, 256), BF),
     "t": ((2, NZ, 16, 256), F32),
     "tz": ((2, NZ, 16, 256), BF),
+    "sum": ((2, 16, 256), F32),
     "rz": ((2, NZ, 16, 256), BF),
 }
 SEMAPHORES = {
-    "ld": 16,
-    "w1": 8,
-    "w2": 6,
+    "ld": 8,
+    "w1": 1,
+    "w2": 1,
     "w3": 8,
-    "wd": 10,
-    "k": 8,
-    "v": 16,
-    "e": 16,
+    "wd": 1,
+    "k": 5,
+    "v": 12,
+    "e": 2,
     "r": 8,
     "f": 4,
     "g": 4,
-    "vg": 16,
-    "vd": 16,
-    "x": 8,
-    "z": 16,
+    "vg": 12,
+    "vd": 4,
+    "x": 6,
+    "z": 2,
 }
+SENDERS = tuple(SEMAPHORES) + ("es",)
 
 
 def kernel(need, doc, emb_h, q_h, k_h, cot_h, yw_h, out, *scratch):
     names = list(BUFFERS)
     b = SimpleNamespace(**dict(zip(names, scratch)))
     rest = scratch[len(names) :]
-    snd = dict(zip(SEMAPHORES, rest[: len(SEMAPHORES)]))
-    rcv = dict(zip(SEMAPHORES, rest[len(SEMAPHORES) :]))
+    rcv, snd = dict(zip(SEMAPHORES, rest)), rest[-1]
 
     y, z = lax.axis_index("cp_0"), lax.axis_index("cp_1")
     c, x = lax.axis_index("cp_2"), lax.axis_index("fs")
@@ -109,25 +110,37 @@
     sibling = dev(cp_2=o)
     following, preceding = dev(cp_0=yn, cp_1=zn), dev(cp_0=yp, cp_1=zp)
 
-    started = []
-
-    def copy(src, dst, kind, k, to):
+    sent = dict.fromkeys(SENDERS, 0)
+    results = []
+
+    def copy(src, dst, kind, k, to, sender=None):
         return pltpu.make_async_remote_copy(
             src_ref=src,
             dst_ref=dst,
-            send_sem=snd[kind].at[k],
+            send_sem=snd.at[SENDERS.index(sender or kind)],
             recv_sem=rcv[kind].at[k],
             device_id=to,
             device_id_type=MESH,
         )
 
-    def send(src, dst, kind, k, to):
-        made = copy(src, dst, kind, k, to)
-        made.start()
-        started.append(made)
+    def prepare(src, dst, kind, k, to, sender=None):
+        sent[sender or kind] += math.prod(src.shape) * jnp.dtype(src.dtype).itemsize
+        return copy(src, dst, kind, k, to, sender)
+
+    def send(*what):
+        prepare(*what).start()
 
     def arrived(dst, kind, k):
         copy(dst, dst, kind, k, sibling).wait_recv()
+
+    def room(size):
+        n = size // (1 << 16)
+        if size % (1 << 16):
+            return b.w.at[0, 0, 0 : size // (1 << 14), :, 0]
+        if n <= 8:
+            return b.ex.at[0, 0:n]
+        rows = next(a for a in (2, 3, 4) if n % a == 0 and n // a <= 8)
+        return b.ex.at[0:rows, 0 : n // rows]
 
     loads = {}
 
@@ -159,7 +172,7 @@
     loads["w0"].wait()
     loads["w1"].wait()
     for d in range(1, NZ):
-        send(mine, mine, "w1", d, dev(cp_1=lax.rem(z + d, NZ)))
+        send(mine, mine, "w1", 0, dev(cp_1=lax.rem(z + d, NZ)))
 
     doc_t = jnp.transpose(jnp.broadcast_to(doc[...], (TOK, TOK)))
     row = lax.broadcasted_iota(jnp.int32, (TOK, TOK), 0) + block * TOK
@@ -185,17 +198,15 @@
 
     loads["emb"].wait()
 
-    for d in range(1, NZ):
-        arrived(mine, "w1", d)
+    arrived(room(7 << 14), "w1", 0)
     first, second = b.w.at[0, y, :, c, x], b.w.at[1, y, :, c, x]
     for d in range(1, 4):
-        send(first, first, "w2", d - 1, dev(cp_0=lax.rem(y + d, NY)))
-        send(second, second, "w2", d + 2, dev(fs=lax.rem(x + d, NX)))
+        send(first, first, "w2", 0, dev(cp_0=lax.rem(y + d, NY)))
+        send(second, second, "w2", 0, dev(fs=lax.rem(x + d, NX)))
 
     lax.fori_loop(0, 8, turn, 0)
 
-    for d in range(6):
-        arrived(first, "w2", d)
+    arrived(room(6 << 16), "w2", 0)
 
     def half_a(xx):
         return b.w.at[0, :, :, c, xx]
@@ -215,7 +226,7 @@
     send(half_b(y), half_b(y), "w3", 3, dev(cp_0=ydn))
 
     send(half_a(x), half_a(x), "wd", 0, sibling)
-    send(half_b(y), half_b(y), "wd", 1, sibling)
+    send(half_b(y), half_b(y), "wd", 0, sibling)
 
     loads["k"].wait()
 
@@ -225,10 +236,9 @@
     def pass_keys(s):
         arrived(keys_at(2, s), "k", s)
         send(keys_at(2, s), keys_at(4, s), "k", 2 + s, following)
-        send(keys_at(2 * c, s), keys_at(1, s), "k", 4 + s, sibling)
-
-    keys_out = [copy(keys_at(0, s), keys_at(2, s), "k", s, following) for s in range(2)]
-    started.extend(keys_out)
+        send(keys_at(2 * c, s), keys_at(1, s), "k", 4, sibling)
+
+    keys_out = [prepare(keys_at(0, s), keys_at(2, s), "k", s, following) for s in range(2)]
 
     @pl.when(z != NZ - 1)
     def _():
@@ -239,33 +249,29 @@
     send(relay_a(xdn, 0), relay_a(xdn, 0), "w3", 4, dev(fs=xup))
     arrived(half_a(x), "w3", 1)
     send(relay_a(xup, 1), relay_a(xup, 1), "w3", 5, dev(fs=xdn))
-    arrived(half_b(y), "w3", 2)
-    send(relay_b(ydn, 0), relay_b(ydn, 0), "w3", 6, dev(cp_0=yup))
     arrived(half_b(y), "w3", 3)
-    send(relay_b(yup, 1), relay_b(yup, 1), "w3", 7, dev(cp_0=ydn))
+    for s in range(2):
+        send(relay_b(yup, s), relay_b(yup, s), "w3", 6 + s, dev(cp_0=ydn))
 
     @pl.when(z == NZ - 1)
     def _():
         for made in keys_out:
             made.start()
 
-    send(half_a(xdn), half_a(xdn), "wd", 2, sibling)
-    send(half_a(xup), half_a(xup), "wd", 3, sibling)
-    send(half_b(ydn), half_b(ydn), "wd", 4, sibling)
-    send(half_b(yup), half_b(yup), "wd", 5, sibling)
+    send(half_a(xdn), half_a(xdn), "wd", 0, sibling)
+    send(half_a(xup), half_a(xup), "wd", 0, sibling)
+    arrived(half_b(y), "w3", 2)
+    send(half_b(ydn), half_b(ydn), "wd", 0, sibling)
+    send(half_b(yup), half_b(yup), "wd", 0, sibling)
     pass_keys(0)
     pass_keys(1)
     loads["q"].wait()
     for s in range(2):
         arrived(relay_a(x, s), "w3", 4 + s)
-        send(relay_a(xop, s), relay_a(xop, s), "wd", 6 + s, sibling)
+        send(relay_a(xop, s), relay_a(xop, s), "wd", 0, sibling)
     for s in range(2):
         arrived(relay_b(y, s), "w3", 6 + s)
-        send(relay_b(yop, s), relay_b(yop, s), "wd", 8 + s, sibling)
-    for s in range(2):
-        arrived(keys_at(4, s), "k", 2 + s)
-        send(keys_at(2 + 2 * c, s), keys_at(3, s), "k", 6 + s, sibling)
-
+        send(relay_b(yop, s), relay_b(yop, s), "wd", 0, sibling)
     def head_probs(hd, carry):
         lanes = pl.ds(pl.multiple_of(hd * HEAD, HEAD), HEAD)
         key_lanes = pl.ds(pl.multiple_of(lax.div(hd, GROUP) * HEAD, HEAD), HEAD)
@@ -282,36 +288,29 @@
             b.p[hd, rows, :] = (weight * (1.0 / total)).astype(BF)
         return carry
 
-    for k in (0, 2, 3):
-        arrived(half_a(x), "wd", k)
-    for k in (1, 4, 5):
-        arrived(half_b(y), "wd", k)
-    for s in range(2):
-        arrived(relay_a(x, s), "wd", 6 + s)
-        arrived(relay_b(y, s), "wd", 8 + s)
-
-    def columns_of(blk):
-        return pl.ds(pl.multiple_of(blk * TOK, TOK), TOK)
-
-    own = x * 2 + c
-    here = b.ex.at[:, :, :, columns_of(own)]
-    kept = pltpu.make_async_copy(b.et.at[:, :, c, x], here, rcv["ld"].at[14])
+    arrived(room(32 << 16), "wd", 0)
+
+    def tokens_of(slot, ys=slice(None)):
+        return b.ex.at[ys, :, :, slot * TOK : slot * TOK + TOK]
+
+    kept = pltpu.make_async_copy(b.et.at[:, :, c, x], tokens_of(0), rcv["ld"].at[7])
     kept.start()
-    send(b.et.at[:, :, o, x], here, "e", 0, sibling)
+    send(b.et.at[:, :, o, x], tokens_of(1), "e", 0, sibling, "es")
     for s, xt in enumerate((xup, xdn)):
         for k, cc in enumerate((c, o)):
             part = b.et.at[2 * s : 2 * s + 2, :, cc, xop]
-            send(part, b.er.at[s, k], "e", 8 + 2 * s + k, dev(fs=xt))
+            send(part, b.er.at[s, k], "e", 1, dev(fs=xt))
     for s, xt in enumerate((xup, xdn)):
         for k, cc in enumerate((c, o)):
-            send(b.et.at[:, :, cc, xt], here, "e", 2 + 2 * s + k, dev(fs=xt, cp_2=cc))
+            there = tokens_of(2 + 2 * s + k)
+            send(b.et.at[:, :, cc, xt], there, "e", 0, dev(fs=xt, cp_2=cc))
 
     def pass_embeds():
-        for s, (xt, xf) in enumerate(((xup, xdn), (xdn, xup))):
+        arrived(b.er, "e", 1)
+        for s, xt in enumerate((xup, xdn)):
             for k, cc in enumerate((c, o)):
-                arrived(b.er.at[s, k], "e", 8 + 2 * s + k)
-                there = b.ex.at[2 * s : 2 * s + 2, :, :, columns_of(xf * 2 + c)]
-                send(b.er.at[s, k], there, "e", 12 + 2 * s + k, dev(fs=xt, cp_2=cc))
+                there = tokens_of(6 + k, slice(2 * s, 2 * s + 2))
+                send(b.er.at[s, k], there, "e", 0, dev(fs=xt, cp_2=cc))
 
     for h in range(2):
         made = jnp.dot(b.emb[...], b.w[h].reshape(4096, 256), preferred_element_type=F32)
@@ -327,11 +326,10 @@
 
     def pass_far(kv):
         arrived(b.vw.at[kv, 4], "v", 4 + kv)
-        send(b.vw.at[kv, 2 + 2 * c], b.vw.at[kv, 3], "v", 12 + kv, sibling)
+        send(b.vw.at[kv, 2 + 2 * c], b.vw.at[kv, 3], "v", 8 + kv, sibling)
 
     def attend(kv):
-        arrived(b.vw.at[kv, 1], "v", 8 + kv)
-        arrived(b.vw.at[kv, 3], "v", 12 + kv)
+        arrived(b.vw.at[kv, 0:2], "v", 8 + kv)
 
         def one(k, carry):
             hd = kv * GROUP + k
@@ -346,8 +344,10 @@
         lax.fori_loop(0, GROUP, one, 0)
 
     for s in range(2):
-        arrived(keys_at(1, s), "k", 4 + s)
-        arrived(keys_at(3, s), "k", 6 + s)
+        arrived(keys_at(4, s), "k", 2 + s)
+        send(keys_at(2 + 2 * c, s), keys_at(3, s), "k", 4, sibling)
+
+    arrived(room(8 << 16), "k", 4)
     loads["cot"].wait()
     lax.fori_loop(0, 8, head_probs, 0)
     pass_near(0)
@@ -414,39 +414,31 @@
         b.go[kv] = (b.dv[kv, 2] + b.r[kv, 1 - c] + b.fi[kv].astype(F32)).astype(BF)
         send(b.go.at[kv], b.gi.at[kv], "g", kv, preceding)
 
-    def vg_at(kv, xx, cc, rows=slice(None)):
+    def vg_at(kv, slot, rows=slice(None)):
         lanes = slice((kv % 2) * HEAD, (kv % 2) * HEAD + HEAD)
-        return b.vg.at[kv // 2, xx * 2 + cc, rows, lanes]
+        return b.vg.at[kv // 2, slot, rows, lanes]
 
     upper, lower = slice(0, 128), slice(128, 256)
 
     def settle(kv):
         arrived(b.gi.at[kv], "g", kv)
         total = b.dv[kv, 0] + b.r[kv, 2 * c] + b.gi[kv].astype(F32)
-        b.vg[kv // 2, x * 2 + c, :, (kv % 2) * HEAD : (kv % 2) * HEAD + HEAD] = total.astype(BF)
-        mine = vg_at(kv, x, c)
-        send(mine, mine, "vg", 4 * kv, dev(fs=xup))
-        send(mine, mine, "vg", 4 * kv + 1, dev(fs=xdn))
-        send(mine, mine, "vd", 4 * kv, sibling)
+        b.vg[kv // 2, 0, :, (kv % 2) * HEAD : (kv % 2) * HEAD + HEAD] = total.astype(BF)
+        send(vg_at(kv, 0), vg_at(kv, 2), "vg", 3 * kv, dev(fs=xup))
+        send(vg_at(kv, 0), vg_at(kv, 4), "vg", 3 * kv + 1, dev(fs=xdn))
+        send(vg_at(kv, 0), vg_at(kv, 1), "vd", kv // 2, sibling)
 
     def relay(kv):
-        arrived(vg_at(kv, x, c), "vg", 4 * kv)
-        part = vg_at(kv, xdn, c, upper)
-        send(part, part, "vg", 4 * kv + 2, dev(fs=xup))
-        send(vg_at(kv, xdn, c), vg_at(kv, xdn, c), "vd", 4 * kv + 1, sibling)
-        arrived(vg_at(kv, x, c), "vg", 4 * kv + 1)
-        part = vg_at(kv, xup, c, lower)
-        send(part, part, "vg", 4 * kv + 3, dev(fs=xdn))
-        send(vg_at(kv, xup, c), vg_at(kv, xup, c), "vd", 4 * kv + 2, sibling)
+        arrived(vg_at(kv, 2), "vg", 3 * kv)
+        send(vg_at(kv, 2, upper), vg_at(kv, 6, upper), "vg", 3 * kv + 2, dev(fs=xup))
+        send(vg_at(kv, 2), vg_at(kv, 3), "vd", kv // 2, sibling)
+        arrived(vg_at(kv, 4), "vg", 3 * kv + 1)
+        send(vg_at(kv, 4, lower), vg_at(kv, 6, lower), "vg", 3 * kv + 2, dev(fs=xdn))
+        send(vg_at(kv, 4), vg_at(kv, 5), "vd", kv // 2, sibling)
 
     def collect(kv):
-        arrived(vg_at(kv, x, c, upper), "vg", 4 * kv + 2)
-        arrived(vg_at(kv, x, c, lower), "vg", 4 * kv + 3)
-        send(vg_at(kv, xop, c), vg_at(kv, xop, c), "vd", 4 * kv + 3, sibling)
-
-    def complete(kv):
-        for k in range(4):
-            arrived(vg_at(kv, x, c), "vd", 4 * kv + k)
+        arrived(vg_at(kv, 6), "vg", 3 * kv + 2)
+        send(vg_at(kv, 6), vg_at(kv, 7), "vd", 2 + kv // 2, sibling)
 
     grads_far(0)
     grads_far(1)
@@ -469,10 +461,7 @@
     grads(3, 0, 1)
     leave_near(3)
     kept.wait()
-    for k in (0, 2, 3, 4, 5):
-        arrived(here, "e", k)
-    for k in range(12, 16):
-        arrived(b.er.at[0, 0], "e", k)
+    arrived(room(28 << 16), "e", 0)
 
     settle(0)
     settle(1)
@@ -480,55 +469,65 @@
     relay(0)
     settle(3)
     relay(1)
-    collect(0)
     relay(2)
-    collect(1)
-    complete(0)
-    complete(1)
+
+    def early(h):
+        arrived(room(6 << 16), "vd", h)
+        b.g[h] = jnp.dot(
+            b.ex[:, :, :, 0 : 6 * TOK].reshape(512, 6 * TOK),
+            b.vg[h, 0:6].reshape(6 * TOK, 256),
+            preferred_element_type=F32,
+        ).reshape(NY, NZ, 16, 256)
 
     def product(h):
-        grad = jnp.dot(
-            b.ex[...].reshape(512, 8 * TOK),
-            b.vg[h].reshape(8 * TOK, 256),
+        arrived(room(2 << 16), "vd", 2 + h)
+        b.g[h] += jnp.dot(
+            b.ex[:, :, :, 6 * TOK : 8 * TOK].reshape(512, 2 * TOK),
+            b.vg[h, 6:8].reshape(2 * TOK, 256),
             preferred_element_type=F32,
-        )
-        b.g[h] = grad.reshape(NY, NZ, 16, 256)
+        ).reshape(NY, NZ, 16, 256)
         b.g1[h] = b.g[h, yop].astype(BF)
-        send(b.g1.at[h, 0:4], b.x1.at[h, 0], "x", 4 * h, dev(cp_0=yup))
-        send(b.g1.at[h, 4:8], b.x1.at[h, 1], "x", 4 * h + 1, dev(cp_0=ydn))
+        send(b.g1.at[h, 0:4], b.x1.at[h, 0], "x", 3 * h, dev(cp_0=yup))
+        send(b.g1.at[h, 4:8], b.x1.at[h, 1], "x", 3 * h + 1, dev(cp_0=ydn))
 
     def across(h):
-        arrived(b.x1.at[h, 0], "x", 4 * h)
+        arrived(b.x1.at[h, 0], "x", 3 * h)
         b.tx[h, 0, 0:4] = (b.g[h, yup, 0:4] + b.x1[h, 0].astype(F32)).astype(BF)
         b.tx[h, 0, 4:8] = b.g[h, yup, 4:8].astype(BF)
-        send(b.tx.at[h, 0], b.x2.at[h, 0], "x", 4 * h + 2, dev(cp_0=yup))
-        arrived(b.x1.at[h, 1], "x", 4 * h + 1)
+        send(b.tx.at[h, 0], b.x2.at[h, 0], "x", 3 * h + 2, dev(cp_0=yup))
+        arrived(b.x1.at[h, 1], "x", 3 * h + 1)
         b.tx[h, 1, 0:4] = b.g[h, ydn, 0:4].astype(BF)
         b.tx[h, 1, 4:8] = (b.g[h, ydn, 4:8] + b.x1[h, 1].astype(F32)).astype(BF)
-        send(b.tx.at[h, 1], b.x2.at[h, 1], "x", 4 * h + 3, dev(cp_0=ydn))
+        send(b.tx.at[h, 1], b.x2.at[h, 1], "x", 3 * h + 2, dev(cp_0=ydn))
 
     def along(h):
-        arrived(b.x2.at[h, 0], "x", 4 * h + 2)
-        arrived(b.x2.at[h, 1], "x", 4 * h + 3)
+        arrived(b.x2.at[h], "x", 3 * h + 2)
         b.t[h] = b.g[h, y] + b.x2[h, 0].astype(F32) + b.x2[h, 1].astype(F32)
         b.tz[h] = b.t[h].astype(BF)
         for d in (4, 3, 5, 2, 6, 1, 7):
             zt = lax.rem(z + d, NZ)
-            send(b.tz.at[h, zt], b.rz.at[h, z], "z", 8 * h + d, dev(cp_1=zt))
+            send(b.tz.at[h, zt], b.rz.at[h, z], "z", h, dev(cp_1=zt))
 
     def finish(h):
+        arrived(b.rz.at[h, 0:7], "z", h)
         total = b.t[h, z]
-        for d in (1, 7, 2, 6, 3, 5, 4):
-            arrived(b.rz.at[h, 0], "z", 8 * h + d)
-            total = total + b.rz[h, lax.rem(z + NZ - d, NZ)].astype(F32)
-        out[:, h * 256 : (h + 1) * 256] = total
-
+        for d in range(1, NZ):
+            total = total + b.rz[h, lax.rem(z + d, NZ)].astype(F32)
+        b.sum[h] = total
+        made = pltpu.make_async_copy(
+            b.sum.at[h], out.at[:, h * 256 : (h + 1) * 256], rcv["ld"].at[h]
+        )
+        made.start()
+        results.append(made)
+
+    early(0)
+    collect(0)
     relay(3)
+    collect(1)
     product(0)
     collect(2)
+    early(1)
     collect(3)
-    complete(2)
-    complete(3)
     product(1)
     across(0)
     across(1)
@@ -537,21 +536,24 @@
     finish(0)
     finish(1)
 
-    for made in started:
-        made.wait_send()
+    for made in results:
+        made.wait()
+    for kind, size in sent.items():
+        if size:
+            copy(room(size), room(size), "w1", 0, sibling, kind).wait_send()
 
 
 def weight_gradient(need_ids, doc_start, embeds, queries, key_heads, cotangent, y_weight):
     any_space = pl.BlockSpec(memory_space=pl.ANY)
     vmem = pl.BlockSpec(memory_space=pltpu.VMEM)
     semaphores = [pltpu.SemaphoreType.DMA((n,)) for n in SEMAPHORES.values()]
+    semaphores.append(pltpu.SemaphoreType.DMA((len(SENDERS),)))
     return pl.pallas_call(
         kernel,
         out_shape=jax.ShapeDtypeStruct((16, 512), F32),
         in_specs=[pl.BlockSpec(memory_space=pltpu.SMEM), vmem] + [any_space] * 5,
-        out_specs=vmem,
+        out_specs=any_space,
         scratch_shapes=[pltpu.VMEM(shape, kind) for shape, kind in BUFFERS.values()]
-        + semaphores
         + semaphores,
         compiler_params=pltpu.CompilerParams(
             collective_id=0, has_side_effects=True, vmem_limit_bytes=58 << 20

time: 117 us -> 101 us (0.86)
  Pallas kernels: 114 us -> 98.2 us
    pallas_call x1, Pallas kernels: 114 us -> 98.2 us  [weight_gradient(): pl.pallas_call(kernel, out_shape=jax.ShapeDtypeStruct((16, 512), F32), in...]
where the time goes in v5:
time: 101 us; the launch traced here: 100 us
  Pallas kernels  98.2 us (97%)
  other arithmetic  1.42 us (1%)
    pallas_call x1, Pallas kernels, weight_gradient(): pl.pallas_call(kernel, out_shape=jax.ShapeDtypeStruct((16, 512), F32), in...  98.2 us

profile of v5, /device:TPU:1, one launch (start us, length us, event | category | flops | bytes accessed | tf_op | source)
XLA Modules:
  0.0 100.4 jit_solution(14477722916383272580)
XLA Ops:
  0.6 0.0 copy-start
  0.6 0.0 copy-start.1
  0.7 0.0 copy-start.2
  0.7 0.0 copy-start.3
  0.7 98.2 %shard_map.129 = f32[16,512]{1,0:T(8,128)} custom-call(s32[1,5]{1,0:T(1,128)} %bitcast.9, s32[1,256]{1,0:T(1,128)} %doc.1, bf16[256,4096]{1,0:T(8,128)(2,1)} %bitcast.5, bf16[256,2048]{1,0:T(8,128)(2,1)} %bitcast.6, bf16[256,512]{1,0:T(8,128)(2,1)} %bitcast.8, bf16[256,2048]{1,0:T(8,128)(2,1)} %bitcast.7, bf16[16,512]{1,0:T(8,128)(2,1)} %yw_h.1), custom_call_target="tpu_custom_call" | custom-call | tf_op jit(solution)/shard_map/pallas_call | solution.py:551
  98.9 0.0 copy-done
  98.9 0.0 copy-done.1
  98.9 0.0 copy-done.2
  98.9 0.0 copy-done.3
  99.0 1.4 %add_convert_fusion = (bf16[16,512]{1,0:T(8,128)(2,1)}, f32[16,512]{1,0:T(8,128)}, f32[16,512]{1,0:T(8,128)}, f32[16,512]{1,0:T(8,128)}) fusion(f32[16,512]{1,0:T(8,128)S(1)} %copy-done.1, f32[16,512]{1,0:T(8,128)S(1)} %copy-done.2, bf16[16,512]{1,0:T(8,128)(2,1)S(1)} %copy-done, f32[16,512]{1,0:T(8,128)} %shard_map.129, f32[16,512]{1,0:T(8,128)S(1)} %copy-done.3), kind=kLoop, calls=%fused_computation.2 | loop fusion | flops 147456 | bytes 262144 | tf_op jit(solution)/shard_map/convert_element_type | solution.py:584
Async XLA Ops:
  0.6 98.3 %copy-start = (bf16[16,512]{1,0:T(8,128)(2,1)S(1)}, bf16[16,512]{1,0:T(8,128)(2,1)}, u32[]{:S(2)}) copy-start(bf16[16,512]{1,0:T(8,128)(2,1)} %yw_h.1) | copy-start | bytes 49156
  0.6 98.3 %copy-start.1 = (f32[16,512]{1,0:T(8,128)S(1)}, f32[16,512]{1,0:T(8,128)}, u32[]{:S(2)}) copy-start(f32[16,512]{1,0:T(8,128)} %param.18) | copy-start | bytes 98308
  0.7 98.3 %copy-start.2 = (f32[16,512]{1,0:T(8,128)S(1)}, f32[16,512]{1,0:T(8,128)}, u32[]{:S(2)}) copy-start(f32[16,512]{1,0:T(8,128)} %param.17) | copy-start | bytes 98308
  0.7 98.3 %copy-start.3 = (f32[16,512]{1,0:T(8,128)S(1)}, f32[16,512]{1,0:T(8,128)}, u32[]{:S(2)}) copy-start(f32[16,512]{1,0:T(8,128)} %param.19) | copy-start | bytes 98308

commit v6 on v5

--- a/solution.py
+++ b/solution.py
@@ -36,13 +36,14 @@
 
 BUFFERS = {
     "emb": ((TOK, 4096), BF),
-    "w": ((2, NY, NZ, 2, NX, 16, 256), BF),
+    "w": ((NY, NZ, 2, NX, 16, 512), BF),
     "q": ((TOK, 2048), BF),
     "kw": ((5, TOK, 512), BF),
     "vw": ((KV, 5, TOK, HEAD), BF),
     "cot": ((TOK, 2048), BF),
     "p": ((16, TOK, SPAN), BF),
-    "s": ((TOK, SPAN), F32),
+    "s0": ((TOK, SPAN), F32),
+    "s1": ((TOK, SPAN), F32),
     "bias": ((TOK, SPAN), F32),
     "att": ((16, TOK, HEAD), F32),
     "sq": ((TOK, HEAD), F32),
@@ -136,7 +137,7 @@
     def room(size):
         n = size // (1 << 16)
         if size % (1 << 16):
-            return b.w.at[0, 0, 0 : size // (1 << 14), :, 0]
+            return b.w.at[0, 0 : size // (1 << 14), 0, 0]
         if n <= 8:
             return b.ex.at[0, 0:n]
         rows = next(a for a in (2, 3, 4) if n % a == 0 and n // a <= 8)
@@ -148,9 +149,8 @@
         loads[name] = pltpu.make_async_copy(src, dst, rcv["ld"].at[len(loads)])
         loads[name].start()
 
-    mine = b.w.at[:, y, z, c, x]
-    load("w0", yw_h.at[:, 0:256], b.w.at[0, y, z, c, x])
-    load("w1", yw_h.at[:, 256:512], b.w.at[1, y, z, c, x])
+    mine = b.w.at[y, z, c, x]
+    load("w", yw_h, mine)
     load("k", k_h, b.kw.at[0])
     load("q", q_h, b.q)
     load("emb", emb_h, b.emb)
@@ -169,8 +169,7 @@
         pl.semaphore_signal(barrier, inc=1, device_id=who, device_id_type=MESH)
     pl.semaphore_wait(barrier, len(partners))
 
-    loads["w0"].wait()
-    loads["w1"].wait()
+    loads["w"].wait()
     for d in range(1, NZ):
         send(mine, mine, "w1", 0, dev(cp_1=lax.rem(z + d, NZ)))
 
@@ -199,7 +198,7 @@
     loads["emb"].wait()
 
     arrived(room(7 << 14), "w1", 0)
-    first, second = b.w.at[0, y, :, c, x], b.w.at[1, y, :, c, x]
+    first, second = b.w.at[y, :, c, x, :, 0:256], b.w.at[y, :, c, x, :, 256:512]
     for d in range(1, 4):
         send(first, first, "w2", 0, dev(cp_0=lax.rem(y + d, NY)))
         send(second, second, "w2", 0, dev(fs=lax.rem(x + d, NX)))
@@ -209,16 +208,16 @@
     arrived(room(6 << 16), "w2", 0)
 
     def half_a(xx):
-        return b.w.at[0, :, :, c, xx]
+        return b.w.at[:, :, c, xx, :, 0:256]
 
     def half_b(yy):
-        return b.w.at[1, yy, :, c, :]
+        return b.w.at[yy, :, c, :, :, 256:512]
 
     def relay_a(xx, s):
-        return b.w.at[0, :, 4 * s : 4 * s + 4, c, xx]
+        return b.w.at[:, 4 * s : 4 * s + 4, c, xx, :, 0:256]
 
     def relay_b(yy, s):
-        return b.w.at[1, yy, 4 * s : 4 * s + 4, c, :]
+        return b.w.at[yy, 4 * s : 4 * s + 4, c, :, :, 256:512]
 
     send(half_a(x), half_a(x), "w3", 0, dev(fs=xup))
     send(half_a(x), half_a(x), "w3", 1, dev(fs=xdn))
@@ -272,20 +271,28 @@
     for s in range(2):
         arrived(relay_b(y, s), "w3", 6 + s)
         send(relay_b(yop, s), relay_b(yop, s), "wd", 0, sibling)
-    def head_probs(hd, carry):
+    def scores(hd, into):
         lanes = pl.ds(pl.multiple_of(hd * HEAD, HEAD), HEAD)
         key_lanes = pl.ds(pl.multiple_of(lax.div(hd, GROUP) * HEAD, HEAD), HEAD)
         keys = b.kw[:, :, key_lanes].reshape(SPAN, HEAD)
-        b.s[...] = lax.dot_general(
+        into[...] = lax.dot_general(
             b.q[:, lanes], keys, (((1,), (1,)), ((), ())), preferred_element_type=F32
         )
+
+    def softmax(hd, held):
         for n in range(8):
             rows = slice(n * 32, n * 32 + 32)
-            score = b.s[rows, :] + b.bias[rows, :]
+            score = held[rows, :] + b.bias[rows, :]
             largest = jnp.max(score, axis=-1, keepdims=True)
             weight = jnp.exp2((score - largest) * EXP2_SCALE)
             total = jnp.sum(weight, axis=-1, keepdims=True)
             b.p[hd, rows, :] = (weight * (1.0 / total)).astype(BF)
+
+    def head_probs(pair, carry):
+        scores(2 * pair + 1, b.s1)
+        softmax(2 * pair, b.s0)
+        scores(jnp.minimum(2 * pair + 2, 15), b.s0)
+        softmax(2 * pair + 1, b.s1)
         return carry
 
     arrived(room(32 << 16), "wd", 0)
@@ -312,12 +319,10 @@
                 there = tokens_of(6 + k, slice(2 * s, 2 * s + 2))
                 send(b.er.at[s, k], there, "e", 0, dev(fs=xt, cp_2=cc))
 
-    for h in range(2):
-        made = jnp.dot(b.emb[...], b.w[h].reshape(4096, 256), preferred_element_type=F32)
-        for k in range(2):
-            kv = 2 * h + k
-            b.vw[kv, 0] = made[:, k * HEAD : (k + 1) * HEAD].astype(BF)
-            send(b.vw.at[kv, 0], b.vw.at[kv, 2], "v", kv, following)
+    made = jnp.dot(b.emb[...], b.w[...].reshape(4096, 512), preferred_element_type=F32)
+    for kv in range(KV):
+        b.vw[kv, 0] = made[:, kv * HEAD : (kv + 1) * HEAD].astype(BF)
+        send(b.vw.at[kv, 0], b.vw.at[kv, 2], "v", kv, following)
 
     def pass_near(kv):
         arrived(b.vw.at[kv, 2], "v", kv)
@@ -331,17 +336,13 @@
     def attend(kv):
         arrived(b.vw.at[kv, 0:2], "v", 8 + kv)
 
-        def one(k, carry):
-            hd = kv * GROUP + k
+        for hd in range(kv * GROUP, kv * GROUP + GROUP):
             values = b.vw[kv].reshape(SPAN, HEAD)
-            made = jnp.dot(b.p[hd], values, preferred_element_type=F32)
-            b.att[hd] = made
-            lanes = pl.ds(pl.multiple_of(hd * HEAD, HEAD), HEAD)
-            b.sq[...] += made * made
-            b.cr[...] += made * b.cot[:, lanes].astype(F32)
-            return carry
-
-        lax.fori_loop(0, GROUP, one, 0)
+            b.att[hd] = jnp.dot(b.p[hd], values, preferred_element_type=F32)
+        for hd in range(kv * GROUP, kv * GROUP + GROUP):
+            lanes = slice(hd * HEAD, hd * HEAD + HEAD)
+            b.sq[...] += b.att[hd] * b.att[hd]
+            b.cr[...] += b.att[hd] * b.cot[:, lanes].astype(F32)
 
     for s in range(2):
         arrived(keys_at(4, s), "k", 2 + s)
@@ -349,17 +350,18 @@
 
     arrived(room(8 << 16), "k", 4)
     loads["cot"].wait()
-    lax.fori_loop(0, 8, head_probs, 0)
+    scores(0, b.s0)
+    lax.fori_loop(0, 4, head_probs, 0)
     pass_near(0)
     pass_near(1)
-    lax.fori_loop(8, 11, head_probs, 0)
+    lax.fori_loop(4, 5, head_probs, 0)
     pass_near(2)
-    lax.fori_loop(11, 13, head_probs, 0)
+    lax.fori_loop(5, 6, head_probs, 0)
     pass_near(3)
     pass_embeds()
-    lax.fori_loop(13, 15, head_probs, 0)
+    lax.fori_loop(6, 7, head_probs, 0)
     pass_far(0)
-    lax.fori_loop(15, 16, head_probs, 0)
+    lax.fori_loop(7, 8, head_probs, 0)
     pass_far(1)
     attend(0)
     pass_far(2)
@@ -384,16 +386,13 @@
     lax.fori_loop(0, 8, norm_rows, 0)
 
     def grads(kv, low, high):
-        def one(d, carry):
-            lanes = pl.ds(pl.multiple_of(d * TOK, TOK), TOK)
+        up = b.og[kv * GROUP : kv * GROUP + GROUP].reshape(GROUP * TOK, HEAD)
+        for d in range(low, high):
+            lanes = slice(d * TOK, d * TOK + TOK)
             part = b.p[kv * GROUP : kv * GROUP + GROUP, :, lanes].reshape(GROUP * TOK, TOK)
-            up = b.og[kv * GROUP : kv * GROUP + GROUP].reshape(GROUP * TOK, HEAD)
             b.dv[kv, d] = lax.dot_general(
                 part, up, (((0,), (0,)), ((), ())), preferred_element_type=F32
             )
-            return carry
-
-        lax.fori_loop(low, high, one, 0)
 
     def grads_far(kv):
         grads(kv, 3, 5)
@@ -473,19 +472,21 @@
 
     def early(h):
         arrived(room(6 << 16), "vd", h)
-        b.g[h] = jnp.dot(
-            b.ex[:, :, :, 0 : 6 * TOK].reshape(512, 6 * TOK),
-            b.vg[h, 0:6].reshape(6 * TOK, 256),
-            preferred_element_type=F32,
-        ).reshape(NY, NZ, 16, 256)
+        for ys in (slice(0, 2), slice(2, 4)):
+            b.g[h, ys] = jnp.dot(
+                b.ex[ys, :, :, 0 : 6 * TOK].reshape(256, 6 * TOK),
+                b.vg[h, 0:6].reshape(6 * TOK, 256),
+                preferred_element_type=F32,
+            ).reshape(2, NZ, 16, 256)
 
     def product(h):
         arrived(room(2 << 16), "vd", 2 + h)
-        b.g[h] += jnp.dot(
-            b.ex[:, :, :, 6 * TOK : 8 * TOK].reshape(512, 2 * TOK),
-            b.vg[h, 6:8].reshape(2 * TOK, 256),
-            preferred_element_type=F32,
-        ).reshape(NY, NZ, 16, 256)
+        for ys in (slice(0, 2), slice(2, 4)):
+            b.g[h, ys] += jnp.dot(
+                b.ex[ys, :, :, 6 * TOK : 8 * TOK].reshape(256, 2 * TOK),
+                b.vg[h, 6:8].reshape(2 * TOK, 256),
+                preferred_element_type=F32,
+            ).reshape(2, NZ, 16, 256)
         b.g1[h] = b.g[h, yop].astype(BF)
         send(b.g1.at[h, 0:4], b.x1.at[h, 0], "x", 3 * h, dev(cp_0=yup))
         send(b.g1.at[h, 4:8], b.x1.at[h, 1], "x", 3 * h + 1, dev(cp_0=ydn))

time: 101 us -> 95.4 us (0.945)
  Pallas kernels: 98.2 us -> 93.1 us
    pallas_call x1, Pallas kernels: 98.2 us -> 93.1 us  [weight_gradient(): pl.pallas_call(kernel, out_shape=jax.ShapeDtypeStruct((16, 512), F32), in...]
where the time goes in v6:
time: 95.4 us; the launch traced here: 95.2 us
  Pallas kernels  93.1 us (98%)
  other arithmetic  1.42 us (1%)
    pallas_call x1, Pallas kernels, weight_gradient(): pl.pallas_call(kernel, out_shape=jax.ShapeDtypeStruct((16, 512), F32), in...  93.1 us

profile of v6, /device:TPU:1, one launch (start us, length us, event | category | flops | bytes accessed | tf_op | source)
XLA Modules:
  0.0 95.2 jit_solution(4554516926418656702)
XLA Ops:
  0.6 0.0 copy-start
  0.6 0.0 copy-start.1
  0.7 0.0 copy-start.2
  0.7 0.0 copy-start.3
  0.7 93.1 %shard_map.129 = f32[16,512]{1,0:T(8,128)} custom-call(s32[1,5]{1,0:T(1,128)} %bitcast.9, s32[1,256]{1,0:T(1,128)} %doc.1, bf16[256,4096]{1,0:T(8,128)(2,1)} %bitcast.5, bf16[256,2048]{1,0:T(8,128)(2,1)} %bitcast.6, bf16[256,512]{1,0:T(8,128)(2,1)} %bitcast.8, bf16[256,2048]{1,0:T(8,128)(2,1)} %bitcast.7, bf16[16,512]{1,0:T(8,128)(2,1)} %yw_h.1), custom_call_target="tpu_custom_call" | custom-call | tf_op jit(solution)/shard_map/pallas_call | solution.py:552
  93.8 0.0 copy-done
  93.8 0.0 copy-done.1
  93.8 0.0 copy-done.2
  93.8 0.0 copy-done.3
  93.8 1.4 %add_convert_fusion = (bf16[16,512]{1,0:T(8,128)(2,1)}, f32[16,512]{1,0:T(8,128)}, f32[16,512]{1,0:T(8,128)}, f32[16,512]{1,0:T(8,128)}) fusion(f32[16,512]{1,0:T(8,128)S(1)} %copy-done.1, f32[16,512]{1,0:T(8,128)S(1)} %copy-done.2, bf16[16,512]{1,0:T(8,128)(2,1)S(1)} %copy-done, f32[16,512]{1,0:T(8,128)} %shard_map.129, f32[16,512]{1,0:T(8,128)S(1)} %copy-done.3), kind=kLoop, calls=%fused_computation.2 | loop fusion | flops 147456 | bytes 262144 | tf_op jit(solution)/shard_map/convert_element_type | solution.py:585
Async XLA Ops:
  0.6 93.1 %copy-start = (bf16[16,512]{1,0:T(8,128)(2,1)S(1)}, bf16[16,512]{1,0:T(8,128)(2,1)}, u32[]{:S(2)}) copy-start(bf16[16,512]{1,0:T(8,128)(2,1)} %yw_h.1) | copy-start | bytes 49156
  0.6 93.1 %copy-start.1 = (f32[16,512]{1,0:T(8,128)S(1)}, f32[16,512]{1,0:T(8,128)}, u32[]{:S(2)}) copy-start(f32[16,512]{1,0:T(8,128)} %param.18) | copy-start | bytes 98308
  0.7 93.1 %copy-start.2 = (f32[16,512]{1,0:T(8,128)S(1)}, f32[16,512]{1,0:T(8,128)}, u32[]{:S(2)}) copy-start(f32[16,512]{1,0:T(8,128)} %param.17) | copy-start | bytes 98308
  0.7 93.1 %copy-start.3 = (f32[16,512]{1,0:T(8,128)S(1)}, f32[16,512]{1,0:T(8,128)}, u32[]{:S(2)}) copy-start(f32[16,512]{1,0:T(8,128)} %param.19) | copy-start | bytes 98308

commit v7 on v6

--- a/solution.py
+++ b/solution.py
@@ -351,8 +351,9 @@
     arrived(room(8 << 16), "k", 4)
     loads["cot"].wait()
     scores(0, b.s0)
-    lax.fori_loop(0, 4, head_probs, 0)
+    lax.fori_loop(0, 3, head_probs, 0)
     pass_near(0)
+    lax.fori_loop(3, 4, head_probs, 0)
     pass_near(1)
     lax.fori_loop(4, 5, head_probs, 0)
     pass_near(2)
@@ -371,19 +372,16 @@
     attend(3)
 
     token_total = TOK * NY * NZ * 2 * NX
-
-    def norm_rows(n, carry):
-        rows = pl.ds(pl.multiple_of(n * 32, 32), 32)
-        mean = jnp.sum(b.sq[rows, :], axis=-1, keepdims=True) / 2048.0 + NORM_EPS
-        inv = 1.0 / jnp.sqrt(mean)
-        inner = jnp.sum(b.cr[rows, :], axis=-1, keepdims=True) / (2048.0 * token_total) * inv
-        factor = inner * inv
-        for hd in range(16):
-            up = b.cot[rows, hd * HEAD : (hd + 1) * HEAD].astype(F32) / token_total
-            b.og[hd, rows, :] = ((up - b.att[hd, rows, :] * factor) * inv).astype(BF)
-        return carry
-
-    lax.fori_loop(0, 8, norm_rows, 0)
+    mean = jnp.sum(b.sq[...], axis=-1, keepdims=True) * (1.0 / 2048.0) + NORM_EPS
+    inv = 1.0 / jnp.sqrt(mean)
+    inner = jnp.sum(b.cr[...], axis=-1, keepdims=True) * (1.0 / (2048.0 * token_total)) * inv
+    b.cr[...] = jnp.broadcast_to(inner * inv, (TOK, HEAD))
+    b.sq[...] = jnp.broadcast_to(inv, (TOK, HEAD))
+
+    def norm_grads(kv):
+        for hd in range(kv * GROUP, kv * GROUP + GROUP):
+            up = b.cot[:, hd * HEAD : (hd + 1) * HEAD].astype(F32) * (1.0 / token_total)
+            b.og[hd] = ((up - b.att[hd] * b.cr[...]) * b.sq[...]).astype(BF)
 
     def grads(kv, low, high):
         up = b.og[kv * GROUP : kv * GROUP + GROUP].reshape(GROUP * TOK, HEAD)
@@ -395,6 +393,7 @@
             )
 
     def grads_far(kv):
+        norm_grads(kv)
         grads(kv, 3, 5)
         send(b.dv.at[kv, 3], b.r.at[kv, 1], "r", 2 * kv + 1, sibling)
 
@@ -462,13 +461,10 @@
     kept.wait()
     arrived(room(28 << 16), "e", 0)
 
-    settle(0)
-    settle(1)
-    settle(2)
-    relay(0)
-    settle(3)
-    relay(1)
-    relay(2)
+    for kv in range(KV):
+        settle(kv)
+    for kv in range(KV):
+        relay(kv)
 
     def early(h):
         arrived(room(6 << 16), "vd", h)
@@ -514,20 +510,14 @@
         total = b.t[h, z]
         for d in range(1, NZ):
             total = total + b.rz[h, lax.rem(z + d, NZ)].astype(F32)
-        b.sum[h] = total
-        made = pltpu.make_async_copy(
-            b.sum.at[h], out.at[:, h * 256 : (h + 1) * 256], rcv["ld"].at[h]
-        )
-        made.start()
-        results.append(made)
+        out[:, h * 256 : (h + 1) * 256] = total
 
     early(0)
     collect(0)
-    relay(3)
     collect(1)
+    early(1)
+    collect(2)
     product(0)
-    collect(2)
-    early(1)
     collect(3)
     product(1)
     across(0)
@@ -537,8 +527,6 @@
     finish(0)
     finish(1)
 
-    for made in results:
-        made.wait()
     for kind, size in sent.items():
         if size:
             copy(room(size), room(size), "w1", 0, sibling, kind).wait_send()
@@ -551,9 +539,9 @@
     semaphores.append(pltpu.SemaphoreType.DMA((len(SENDERS),)))
     return pl.pallas_call(
         kernel,
-        out_shape=jax.ShapeDtypeStruct((16, 512), F32),
+        out_shape=pltpu.VMEM((16, 512), F32),
         in_specs=[pl.BlockSpec(memory_space=pltpu.SMEM), vmem] + [any_space] * 5,
-        out_specs=any_space,
+        out_specs=vmem,
         scratch_shapes=[pltpu.VMEM(shape, kind) for shape, kind in BUFFERS.values()]
         + semaphores,
         compiler_params=pltpu.CompilerParams(

time: 95.4 us -> 91.7 us (0.961)
  Pallas kernels: 93.1 us -> 90.1 us
    pallas_call x1, Pallas kernels: 93.1 us -> 90.1 us  [weight_gradient(): pl.pallas_call(kernel, out_shape=pltpu.VMEM((16, 512), F32), in_specs=[pl...]
where the time goes in v7:
time: 91.7 us; the launch traced here: 91.5 us
  Pallas kernels  90.1 us (98%)
    pallas_call x1, Pallas kernels, weight_gradient(): pl.pallas_call(kernel, out_shape=pltpu.VMEM((16, 512), F32), in_specs=[pl...  90.1 us

profile of v7, /device:TPU:1, one launch (start us, length us, event | category | flops | bytes accessed | tf_op | source)
XLA Modules:
  0.0 91.5 jit_solution(4680669300973300790)
XLA Ops:
  0.6 0.0 copy-start
  0.6 0.0 copy-start.1
  0.7 0.0 copy-start.2
  0.7 0.0 copy-start.3
  0.7 90.1 %shard_map.129 = f32[16,512]{1,0:T(8,128)S(1)} custom-call(s32[1,5]{1,0:T(1,128)} %bitcast.9, s32[1,256]{1,0:T(1,128)} %doc.1, bf16[256,4096]{1,0:T(8,128)(2,1)} %bitcast.5, bf16[256,2048]{1,0:T(8,128)(2,1)} %bitcast.6, bf16[256,512]{1,0:T(8,128)(2,1)} %bitcast.8, bf16[256,2048]{1,0:T(8,128)(2,1)} %bitcast.7, bf16[16,512]{1,0:T(8,128)(2,1)} %yw_h.1), custom_call_target="tpu_custom_call" | custom-call | tf_op jit(solution)/shard_map/pallas_call | solution.py:540
  90.8 0.0 copy-done
  90.8 0.0 copy-done.1
  90.8 0.0 copy-done.2
  90.9 0.0 copy-done.3
  90.9 0.7 add_convert_fusion
Async XLA Ops:
  0.6 90.2 %copy-start = (bf16[16,512]{1,0:T(8,128)(2,1)S(1)}, bf16[16,512]{1,0:T(8,128)(2,1)}, u32[]{:S(2)}) copy-start(bf16[16,512]{1,0:T(8,128)(2,1)} %yw_h.1) | copy-start | bytes 49156
  0.6 90.2 %copy-start.1 = (f32[16,512]{1,0:T(8,128)S(1)}, f32[16,512]{1,0:T(8,128)}, u32[]{:S(2)}) copy-start(f32[16,512]{1,0:T(8,128)} %param.18) | copy-start | bytes 98308
  0.7 90.2 %copy-start.2 = (f32[16,512]{1,0:T(8,128)S(1)}, f32[16,512]{1,0:T(8,128)}, u32[]{:S(2)}) copy-start(f32[16,512]{1,0:T(8,128)} %param.17) | copy-start | bytes 98308
  0.7 90.2 %copy-start.3 = (f32[16,512]{1,0:T(8,128)S(1)}, f32[16,512]{1,0:T(8,128)}, u32[]{:S(2)}) copy-start(f32[16,512]{1,0:T(8,128)} %param.19) | copy-start | bytes 98308

commit v8 on v7

--- a/solution.py
+++ b/solution.py
@@ -232,45 +232,69 @@
     def keys_at(d, s):
         return b.kw.at[d, 128 * s : 128 * s + 128]
 
-    def pass_keys(s):
-        arrived(keys_at(2, s), "k", s)
-        send(keys_at(2, s), keys_at(4, s), "k", 2 + s, following)
-        send(keys_at(2 * c, s), keys_at(1, s), "k", 4, sibling)
-
-    keys_out = [prepare(keys_at(0, s), keys_at(2, s), "k", s, following) for s in range(2)]
-
-    @pl.when(z != NZ - 1)
-    def _():
-        for made in keys_out:
-            made.start()
+    for s in range(2):
+        send(keys_at(0, s), keys_at(2, s), "k", s, following)
+    keys_on = [
+        (
+            prepare(keys_at(2, s), keys_at(4, s), "k", 2 + s, following),
+            prepare(keys_at(2 * c, s), keys_at(1, s), "k", 4, sibling),
+        )
+        for s in range(2)
+    ]
+
+    def pass_keys():
+        for s in range(2):
+            arrived(keys_at(2, s), "k", s)
+            for made in keys_on[s]:
+                made.start()
 
     arrived(half_a(x), "w3", 0)
     send(relay_a(xdn, 0), relay_a(xdn, 0), "w3", 4, dev(fs=xup))
     arrived(half_a(x), "w3", 1)
     send(relay_a(xup, 1), relay_a(xup, 1), "w3", 5, dev(fs=xdn))
-    arrived(half_b(y), "w3", 3)
-    for s in range(2):
-        send(relay_b(yup, s), relay_b(yup, s), "w3", 6 + s, dev(cp_0=ydn))
-
-    @pl.when(z == NZ - 1)
+    up_0 = prepare(relay_b(ydn, 0), relay_b(ydn, 0), "w3", 6, dev(cp_0=yup))
+    down_0 = copy(relay_b(yup, 0), relay_b(yup, 0), "w3", 6, dev(cp_0=ydn))
+    down_1 = prepare(relay_b(yup, 1), relay_b(yup, 1), "w3", 7, dev(cp_0=ydn))
+
+    @pl.when(z != 0)
     def _():
-        for made in keys_out:
-            made.start()
+        arrived(half_b(y), "w3", 2)
+        up_0.start()
+        arrived(half_b(y), "w3", 3)
+        down_1.start()
+
+    @pl.when(z == 0)
+    def _():
+        arrived(half_b(y), "w3", 3)
+        down_0.start()
+        down_1.start()
 
     send(half_a(xdn), half_a(xdn), "wd", 0, sibling)
     send(half_a(xup), half_a(xup), "wd", 0, sibling)
-    arrived(half_b(y), "w3", 2)
+    send(half_b(yup), half_b(yup), "wd", 0, sibling)
+
+    @pl.when(z != NZ - 1)
+    def _():
+        pass_keys()
+
+    @pl.when(z == 0)
+    def _():
+        arrived(half_b(y), "w3", 2)
+
     send(half_b(ydn), half_b(ydn), "wd", 0, sibling)
-    send(half_b(yup), half_b(yup), "wd", 0, sibling)
-    pass_keys(0)
-    pass_keys(1)
     loads["q"].wait()
     for s in range(2):
         arrived(relay_a(x, s), "w3", 4 + s)
         send(relay_a(xop, s), relay_a(xop, s), "wd", 0, sibling)
+
+    @pl.when(z == NZ - 1)
+    def _():
+        pass_keys()
+
     for s in range(2):
         arrived(relay_b(y, s), "w3", 6 + s)
         send(relay_b(yop, s), relay_b(yop, s), "wd", 0, sibling)
+
     def scores(hd, into):
         lanes = pl.ds(pl.multiple_of(hd * HEAD, HEAD), HEAD)
         key_lanes = pl.ds(pl.multiple_of(lax.div(hd, GROUP) * HEAD, HEAD), HEAD)

time: 91.7 us -> 90.3 us (0.985)
  Pallas kernels: 90.1 us -> 88.8 us
    pallas_call x1, Pallas kernels: 90.1 us -> 88.8 us  [weight_gradient(): pl.pallas_call(kernel, out_shape=pltpu.VMEM((16, 512), F32), in_specs=[pl...]
where the time goes in v8:
time: 90.3 us; the launch traced here: 90.2 us
  Pallas kernels  88.8 us (98%)
    pallas_call x1, Pallas kernels, weight_gradient(): pl.pallas_call(kernel, out_shape=pltpu.VMEM((16, 512), F32), in_specs=[pl...  88.8 us

profile of v8, /device:TPU:1, one launch (start us, length us, event | category | flops | bytes accessed | tf_op | source)
XLA Modules:
  0.0 90.2 jit_solution(14459811779268727815)
XLA Ops:
  0.6 0.0 copy-start
  0.6 0.0 copy-start.1
  0.7 0.0 copy-start.2
  0.7 0.0 copy-start.3
  0.7 88.8 %shard_map.129 = f32[16,512]{1,0:T(8,128)S(1)} custom-call(s32[1,5]{1,0:T(1,128)} %bitcast.9, s32[1,256]{1,0:T(1,128)} %doc.1, bf16[256,4096]{1,0:T(8,128)(2,1)} %bitcast.5, bf16[256,2048]{1,0:T(8,128)(2,1)} %bitcast.6, bf16[256,512]{1,0:T(8,128)(2,1)} %bitcast.8, bf16[256,2048]{1,0:T(8,128)(2,1)} %bitcast.7, bf16[16,512]{1,0:T(8,128)(2,1)} %yw_h.1), custom_call_target="tpu_custom_call" | custom-call | tf_op jit(solution)/shard_map/pallas_call | solution.py:564
  89.5 0.0 copy-done
  89.5 0.0 copy-done.1
  89.5 0.0 copy-done.2
  89.5 0.0 copy-done.3
  89.5 0.7 add_convert_fusion
Async XLA Ops:
  0.6 88.8 %copy-start = (bf16[16,512]{1,0:T(8,128)(2,1)S(1)}, bf16[16,512]{1,0:T(8,128)(2,1)}, u32[]{:S(2)}) copy-start(bf16[16,512]{1,0:T(8,128)(2,1)} %yw_h.1) | copy-start | bytes 49156
  0.6 88.8 %copy-start.1 = (f32[16,512]{1,0:T(8,128)S(1)}, f32[16,512]{1,0:T(8,128)}, u32[]{:S(2)}) copy-start(f32[16,512]{1,0:T(8,128)} %param.18) | copy-start | bytes 98308
  0.7 88.8 %copy-start.2 = (f32[16,512]{1,0:T(8,128)S(1)}, f32[16,512]{1,0:T(8,128)}, u32[]{:S(2)}) copy-start(f32[16,512]{1,0:T(8,128)} %param.17) | copy-start | bytes 98308
  0.7 88.8 %copy-start.3 = (f32[16,512]{1,0:T(8,128)S(1)}, f32[16,512]{1,0:T(8,128)}, u32[]{:S(2)}) copy-start(f32[16,512]{1,0:T(8,128)} %param.19) | copy-start | bytes 98308

commit v9 on v8

--- a/solution.py
+++ b/solution.py
@@ -273,15 +273,16 @@
     send(half_a(xup), half_a(xup), "wd", 0, sibling)
     send(half_b(yup), half_b(yup), "wd", 0, sibling)
 
+    behind = prepare(half_b(ydn), half_b(ydn), "wd", 0, sibling)
+
+    @pl.when(z != 0)
+    def _():
+        behind.start()
+
     @pl.when(z != NZ - 1)
     def _():
         pass_keys()
 
-    @pl.when(z == 0)
-    def _():
-        arrived(half_b(y), "w3", 2)
-
-    send(half_b(ydn), half_b(ydn), "wd", 0, sibling)
     loads["q"].wait()
     for s in range(2):
         arrived(relay_a(x, s), "w3", 4 + s)
@@ -294,6 +295,11 @@
     for s in range(2):
         arrived(relay_b(y, s), "w3", 6 + s)
         send(relay_b(yop, s), relay_b(yop, s), "wd", 0, sibling)
+
+    @pl.when(z == 0)
+    def _():
+        arrived(half_b(y), "w3", 2)
+        behind.start()
 
     def scores(hd, into):
         lanes = pl.ds(pl.multiple_of(hd * HEAD, HEAD), HEAD)

time: 90.3 us -> 90.3 us (level)
  no operation moved by 1% of the time
where the time goes in v9:
time: 90.3 us; the launch traced here: 90.2 us
  Pallas kernels  88.8 us (98%)
    pallas_call x1, Pallas kernels, weight_gradient(): pl.pallas_call(kernel, out_shape=pltpu.VMEM((16, 512), F32), in_specs=[pl...  88.8 us

profile of v9, /device:TPU:1, one launch (start us, length us, event | category | flops | bytes accessed | tf_op | source)
XLA Modules:
  0.0 90.2 jit_solution(15812263437393425087)
XLA Ops:
  0.6 0.0 copy-start
  0.6 0.0 copy-start.1
  0.7 0.0 copy-start.2
  0.7 0.0 copy-start.3
  0.7 88.8 %shard_map.129 = f32[16,512]{1,0:T(8,128)S(1)} custom-call(s32[1,5]{1,0:T(1,128)} %bitcast.9, s32[1,256]{1,0:T(1,128)} %doc.1, bf16[256,4096]{1,0:T(8,128)(2,1)} %bitcast.5, bf16[256,2048]{1,0:T(8,128)(2,1)} %bitcast.6, bf16[256,512]{1,0:T(8,128)(2,1)} %bitcast.8, bf16[256,2048]{1,0:T(8,128)(2,1)} %bitcast.7, bf16[16,512]{1,0:T(8,128)(2,1)} %yw_h.1), custom_call_target="tpu_custom_call" | custom-call | tf_op jit(solution)/shard_map/pallas_call | solution.py:570
  89.5 0.0 copy-done
  89.5 0.0 copy-done.1
  89.5 0.0 copy-done.2
  89.5 0.0 copy-done.3
  89.5 0.7 add_convert_fusion
Async XLA Ops:
  0.6 88.8 %copy-start = (bf16[16,512]{1,0:T(8,128)(2,1)S(1)}, bf16[16,512]{1,0:T(8,128)(2,1)}, u32[]{:S(2)}) copy-start(bf16[16,512]{1,0:T(8,128)(2,1)} %yw_h.1) | copy-start | bytes 49156
  0.6 88.8 %copy-start.1 = (f32[16,512]{1,0:T(8,128)S(1)}, f32[16,512]{1,0:T(8,128)}, u32[]{:S(2)}) copy-start(f32[16,512]{1,0:T(8,128)} %param.18) | copy-start | bytes 98308
  0.7 88.8 %copy-start.2 = (f32[16,512]{1,0:T(8,128)S(1)}, f32[16,512]{1,0:T(8,128)}, u32[]{:S(2)}) copy-start(f32[16,512]{1,0:T(8,128)} %param.17) | copy-start | bytes 98308
  0.7 88.8 %copy-start.3 = (f32[16,512]{1,0:T(8,128)S(1)}, f32[16,512]{1,0:T(8,128)}, u32[]{:S(2)}) copy-start(f32[16,512]{1,0:T(8,128)} %param.19) | copy-start | bytes 98308

commit v10 on v9

--- a/solution.py
+++ b/solution.py
@@ -542,13 +542,13 @@
             total = total + b.rz[h, lax.rem(z + d, NZ)].astype(F32)
         out[:, h * 256 : (h + 1) * 256] = total
 
-    early(0)
     collect(0)
     collect(1)
+    early(0)
+    collect(2)
     early(1)
-    collect(2)
+    collect(3)
     product(0)
-    collect(3)
     product(1)
     across(0)
     across(1)

time: 90.3 us -> 90.8 us (level)
  no operation moved by 1% of the time
where the time goes in v10:
time: 90.8 us; the launch traced here: 90.3 us
  Pallas kernels  88.9 us (98%)
    pallas_call x1, Pallas kernels, weight_gradient(): pl.pallas_call(kernel, out_shape=pltpu.VMEM((16, 512), F32), in_specs=[pl...  88.9 us

profile of v10, /device:TPU:1, one launch (start us, length us, event | category | flops | bytes accessed | tf_op | source)
XLA Modules:
  0.0 90.3 jit_solution(16092325119793514447)
XLA Ops:
  0.6 0.0 copy-start
  0.6 0.0 copy-start.1
  0.7 0.0 copy-start.2
  0.7 0.0 copy-start.3
  0.7 88.9 %shard_map.129 = f32[16,512]{1,0:T(8,128)S(1)} custom-call(s32[1,5]{1,0:T(1,128)} %bitcast.9, s32[1,256]{1,0:T(1,128)} %doc.1, bf16[256,4096]{1,0:T(8,128)(2,1)} %bitcast.5, bf16[256,2048]{1,0:T(8,128)(2,1)} %bitcast.6, bf16[256,512]{1,0:T(8,128)(2,1)} %bitcast.8, bf16[256,2048]{1,0:T(8,128)(2,1)} %bitcast.7, bf16[16,512]{1,0:T(8,128)(2,1)} %yw_h.1), custom_call_target="tpu_custom_call" | custom-call | tf_op jit(solution)/shard_map/pallas_call | solution.py:570
  89.6 0.0 copy-done
  89.6 0.0 copy-done.1
  89.6 0.0 copy-done.2
  89.6 0.0 copy-done.3
  89.6 0.7 add_convert_fusion
Async XLA Ops:
  0.6 88.9 %copy-start = (bf16[16,512]{1,0:T(8,128)(2,1)S(1)}, bf16[16,512]{1,0:T(8,128)(2,1)}, u32[]{:S(2)}) copy-start(bf16[16,512]{1,0:T(8,128)(2,1)} %yw_h.1) | copy-start | bytes 49156
  0.6 88.9 %copy-start.1 = (f32[16,512]{1,0:T(8,128)S(1)}, f32[16,512]{1,0:T(8,128)}, u32[]{:S(2)}) copy-start(f32[16,512]{1,0:T(8,128)} %param.18) | copy-start | bytes 98308
  0.7 88.9 %copy-start.2 = (f32[16,512]{1,0:T(8,128)S(1)}, f32[16,512]{1,0:T(8,128)}, u32[]{:S(2)}) copy-start(f32[16,512]{1,0:T(8,128)} %param.17) | copy-start | bytes 98308
  0.7 88.9 %copy-start.3 = (f32[16,512]{1,0:T(8,128)S(1)}, f32[16,512]{1,0:T(8,128)}, u32[]{:S(2)}) copy-start(f32[16,512]{1,0:T(8,128)} %param.19) | copy-start | bytes 98308
